TPU v7x, 512 devices: a 4x2x32 block of a 4x8x32 slice. The times are simulated.
512 devices in a mesh: parts: 2 (over y), step: 32 (over z), frame: 4 (over x), head: 2 (over core).
Axes of the slice: x: 4, y: 2, z: 32, core: 2. Of those that a mesh axis runs over, the one named last changes fastest.
The devices are a block of a 4x8x32 slice.
Arguments:
- start_noise: float32 [32, 512], P('parts', 'frame'), parts along dimension 0, may hold values from -6 to 6
- position: bfloat16 [512, 1152], P('frame'), may hold values from -6 to 6
- time_table: bfloat16 [128, 1152], replicated, may hold values from -6 to 6
- time_index: int32 [32], P('step'), may hold values from 0 to 127
- sched_index: int32 [32], P('step'), may hold values from 0 to 127
- coef_keep: float32 [128], replicated, may hold values from -0.06 to -0.01
- coef_noise: float32 [128], replicated, may hold values from 0.03 to 0.12
- w_in: bfloat16 [16, 1152], replicated, may hold values from -1.5 to 1.5
- norm_gain: float32 [1152], replicated, may hold values from 0.5 to 1.5
- w_qkv: bfloat16 [1152, 3, 1152], P('step', None, 'head'), may hold values from -4 to 4
- w_proj: bfloat16 [1152, 1152], P('step', 'head'), may hold values from -0.1875 to 0.1875
- w_final: bfloat16 [16, 1152], replicated, may hold values from -0.1875 to 0.1875
Outputs:
- trajectory: float32 [32, 32, 512], P('step', 'parts', 'frame'), parts along dimension 1
- residual_norms: float32 [8], P('parts'), parts along dimension 0
There are 2 independent parts, one for each index of `parts`. A program takes and returns all parts, laid end to end along the dimension named above; an argument that names none is the same for every part. Nothing has to cross between parts.
All inputs are finite; a program needn't handle non-finite values.
Results may differ from a plain program's by a relative error of at most 0.0044.
Values may be sent and summed in bfloat16 or wider, within the bound.
No kernel may reach another device: no remote copies, remote signals or barrier semaphores. Data moves between devices by JAX's collectives and lax.ppermute only.
A program may use at most 64 MiB of HBM per device.

v0:
```python
import math

import jax
import jax.numpy as jnp
from jax import lax
from jax.sharding import PartitionSpec as P

HDIM = 72
ITERS = 4


def in_one_piece(arrays, axis, dim, along):
    columns = [a.reshape(*a.shape[:along], -1) for a in arrays]
    both = jnp.concatenate(columns, axis=along)
    result, at, outs = (lax.all_gather(both, axis, axis=dim, tiled=True), 0, [])
    for a, column in zip(arrays, columns):
        slab = result[..., at : at + column.shape[along]]
        outs.append(slab.reshape(*slab.shape[:along], *a.shape[along:]))
        at += column.shape[along]
    return tuple(outs)


def sent_to_all(value, axis):
    count = lax.axis_size(axis)
    return lax.all_to_all(
        jnp.broadcast_to(value[None], (count, *value.shape)), axis, 0, 0, tiled=True
    )


def joined_along(pieces, dim):
    pieces = jnp.moveaxis(pieces, 0, dim)
    dims = pieces.shape
    return pieces.reshape(*dims[:dim], dims[dim] * dims[dim + 1], *dims[dim + 2 :])


def collect(value, axis, dim):
    pieces = sent_to_all(value, axis)
    return joined_along(pieces, dim)


def of_everyone(value, axis):
    everything = sent_to_all(value, axis)
    return jnp.sum(everything, axis=0)


def joined_by_halves(pieces, combine):
    while len(jax.tree.leaves(pieces)[0]) > 1:
        pieces = jax.vmap(combine)(*(pieces[side::2] for side in (0, 1)))
    return pieces[0]


def prefix(value, axis, combine, identity):
    count, here = (lax.axis_size(axis), lax.axis_index(axis))
    passed = jnp.arange(count) < here

    def kept(part, zero, own):
        part = jnp.where(
            passed.reshape(-1, *(1 for _ in own.shape)), part, jnp.asarray(zero, own.dtype)
        )
        return part

    pieces = sent_to_all(value, axis)
    return joined_by_halves(kept(pieces, identity, value), combine)


def over_axes(value, axes):
    for axis in axes:
        value = lax.psum(value, axis)
    return value


def add_terms(first, second):
    return first + second


def local(
    start_noise,
    position,
    time_table,
    time_index,
    sched_index,
    coef_keep,
    coef_noise,
    w_in,
    norm_gain,
    w_qkv,
    w_proj,
    w_final,
):
    w_qkv_all, w_proj_all = in_one_piece((w_qkv, w_proj), "step", 0, 1)
    batch_steps = time_index.shape[0]
    row_count = start_noise.shape[1]
    table_rows = time_table.shape[0]
    pick_time = (time_index[:, None] == jnp.arange(table_rows)[None, :]).astype(jnp.bfloat16)
    time_embed = jnp.dot(pick_time, time_table, preferred_element_type=jnp.float32)
    pick_sched = (sched_index[:, None] == jnp.arange(table_rows)[None, :]).astype(jnp.float32)
    keep_rate = jnp.sum(pick_sched * coef_keep[None, :], axis=1)
    noise_rate = jnp.sum(pick_sched * coef_noise[None, :], axis=1)
    heads_local = w_qkv_all.shape[2] // HDIM
    cell_count = (
        batch_steps
        * lax.axis_size("step")
        * start_noise.shape[0]
        * row_count
        * lax.axis_size("frame")
    )
    states = start_noise[None]
    drift_term = jnp.zeros_like(states)
    square_list = []
    for iteration in range(ITERS):
        latent_bf = states.astype(jnp.bfloat16)
        hidden = (
            jnp.einsum("bcr,cd->brd", latent_bf, w_in, preferred_element_type=jnp.float32)
            + position
            + time_embed[:, None, :]
        )
        normed = (
            hidden * lax.rsqrt(jnp.mean(hidden * hidden, axis=2, keepdims=True) + 1e-06) * norm_gain
        ).astype(jnp.bfloat16)
        projected = jnp.einsum(
            "brd,dkq->brkq", normed, w_qkv_all, preferred_element_type=jnp.float32
        ).astype(jnp.bfloat16)
        queries = projected[:, :, 0].reshape(batch_steps, row_count, heads_local, HDIM)
        score_scale = 1.0 / math.sqrt(HDIM)
        keys_values = projected[:, :, 1:3]
        piece = collect(keys_values, "frame", 1)
        top_old = jnp.full((batch_steps, heads_local, row_count), -1e30, jnp.float32)
        piece_rows = piece.shape[1]
        keys_blk = piece[:, :, 0].reshape(batch_steps, piece_rows, heads_local, HDIM)
        values_blk = piece[:, :, 1].reshape(batch_steps, piece_rows, heads_local, HDIM)
        scores = (
            jnp.einsum("bqhe,bkhe->bhqk", queries, keys_blk, preferred_element_type=jnp.float32)
            * score_scale
        )
        top_new = jnp.maximum(top_old, jnp.max(scores, axis=3))
        weights_exp = jnp.exp(scores - top_new[:, :, :, None])
        total_new = jnp.sum(weights_exp, axis=3)
        update = jnp.einsum(
            "bhqk,bkhe->bqhe",
            weights_exp.astype(jnp.bfloat16),
            values_blk,
            preferred_element_type=jnp.float32,
        )
        accum = update
        top_final, total_final, accum = (top_new, total_new, accum)
        attended = accum / jnp.transpose(total_final, (0, 2, 1))[:, :, :, None]
        attn_mixed = attended.reshape(batch_steps, row_count, heads_local * HDIM).astype(
            jnp.bfloat16
        )
        partial_value = jnp.einsum(
            "brq,dq->brd", attn_mixed, w_proj_all, preferred_element_type=jnp.float32
        )
        head_total = of_everyone(partial_value, "head")
        joined = (hidden + head_total).astype(jnp.bfloat16)
        predicted = jnp.einsum("cd,brd->bcr", w_final, joined, preferred_element_type=jnp.float32)
        drift_term = keep_rate[:, None, None] * states + noise_rate[:, None, None] * predicted
        local_incl = jnp.cumsum(drift_term, axis=0)
        local_total = local_incl[-1]
        earlier = prefix(local_total, "step", add_terms, jnp.zeros_like(local_total))
        before = earlier[None] + (local_incl - drift_term)
        new_states = start_noise[None] + before
        change = new_states - states
        square_sum = jnp.sum(change * change)
        square_list.append(square_sum)
        states = new_states
    summed_all = over_axes(jnp.stack(square_list), ("step", "frame"))
    residual_norms = jnp.sqrt(summed_all / cell_count + 1e-06)
    trajectory = states + drift_term
    return (trajectory, residual_norms)


def solution(mesh):
    return jax.shard_map(
        local,
        mesh=mesh,
        in_specs=(
            P("parts", "frame"),
            P("frame", None),
            P(),
            P("step"),
            P("step"),
            P(),
            P(),
            P(),
            P(),
            P("step", None, "head"),
            P("step", "head"),
            P(),
        ),
        out_specs=(P("step", "parts", "frame"), P("parts")),
        check_vma=False,
    )
```

profile of v0, /device:TPU:34, one launch (start us, length us, event | category | flops | bytes accessed | tf_op | source)
XLA Modules:
  0.0 601.3 jit_solution(11817579588621640000)
XLA Ops:
  7.3 1.0 copy.25
  8.4 1.6 maximum_bitcast_fusion
  10.9 1.4 multiply_reduce_fusion.7
  12.3 167.9 %all-gather.3.cloned.1.call-done = bf16[32,36,2304]{2,1,0:T(8,128)(2,1)} async-done(((bf16[1,36,2304]{2,1,0:T(8,128)(2,1)}), bf16[32,36,2304]{2,1,0:T(8,128)(2,1)}) %all-gather.3.cloned.1.call-update) | async-done | bytes 5308432 | tf_op jit(solution)/shard_map/all_gather | solution.py:15
  180.2 7.7 %reshape.409 = bf16[1152,2304]{1,0:T(8,128)(2,1)} reshape(bf16[32,36,2304]{2,1,0:T(8,128)(2,1)} %all-gather.3.cloned.1.call-done) | data formatting | bytes 10616832
  188.0 4.5 slice.240
  192.4 6.5 %copy.26 = bf16[1152,1728]{0,1:T(8,128)(2,1)} copy(bf16[1152,1728]{1,0:T(8,128)(2,1)} %slice.240) | data formatting | bytes 7962624 | tf_op jit(solution)/shard_map/slice | solution.py:17
  198.9 3.4 fusion.12
  202.4 1.2 broadcast_in_dim.69
  203.6 4.6 all-to-all-start
  210.1 8.2 %all-to-all-done = bf16[4,1,128,2,576]{2,4,3,1,0:T(8,128)(2,1)S(1)} async-done(((bf16[4,1,128,2,576]{2,4,3,1,0:T(8,128)(2,1)}), bf16[4,1,128,2,576]{2,4,3,1,0:T(8,128)(2,1)S(1)}, u32[]{:S(2)}, u32[]{:S(2)}) %all-to-all-start) | async-done | bytes 1179680 | tf_op jit(solution)/shard_map/all_to_all | solution.py:25
  219.7 0.7 fusion.25
  220.4 2.2 fusion.50
  222.7 4.7 all_to_all.60
  227.6 1.5 fusion.23
  229.1 0.8 broadcast_in_dim.72
  229.9 12.9 %all-to-all-start.2 = ((f32[32,16,128]{2,1,0:T(8,128)}), f32[32,16,128]{2,1,0:T(8,128)S(1)}, u32[]{:S(2)}, u32[]{:S(2)}) async-start(f32[32,16,128]{2,1,0:T(8,128)} %broadcast_in_dim.72), calls=%async_computation.2 | async-start | bytes 524288 | tf_op jit(solution)/shard_map/all_to_all | solution.py:25
  242.8 42.1 %all-to-all-done.2 = f32[32,16,128]{2,1,0:T(8,128)S(1)} async-done(((f32[32,16,128]{2,1,0:T(8,128)}), f32[32,16,128]{2,1,0:T(8,128)S(1)}, u32[]{:S(2)}, u32[]{:S(2)}) %all-to-all-start.2) | async-done | bytes 262176 | tf_op jit(solution)/shard_map/all_to_all | solution.py:25
  285.6 3.4 fusion.13
  289.0 1.2 broadcast_in_dim.75
  290.2 5.0 all-to-all-start.3
  295.2 14.6 %all-to-all-done.3 = bf16[4,1,128,2,576]{2,4,3,1,0:T(8,128)(2,1)S(1)} async-done(((bf16[4,1,128,2,576]{2,4,3,1,0:T(8,128)(2,1)}), bf16[4,1,128,2,576]{2,4,3,1,0:T(8,128)(2,1)S(1)}, u32[]{:S(2)}, u32[]{:S(2)}) %all-to-all-start.3) | async-done | bytes 1179680 | tf_op jit(solution)/shard_map/all_to_all | solution.py:25
  311.8 2.2 fusion.48
  314.1 4.7 all_to_all.61
  319.0 1.7 fusion.21
  320.8 46.5 %all_to_all.62 = f32[32,16,128]{2,1,0:T(8,128)S(1)} all-to-all(f32[32,16,128]{2,1,0:T(8,128)S(1)} %broadcast_in_dim.78), channel_id=1, replica_groups=mesh['parts'=2,'step'=32,'frame'=4,'head'=2] {'step'}, dimensions={0} | all-to-all | bytes 524288 | tf_op jit(solution)/shard_map/all_to_all | solution.py:25
  367.8 1.3 fusion.14
  369.2 1.2 broadcast_in_dim.80
  370.4 5.0 all-to-all-start.6
  375.3 15.1 %all-to-all-done.6 = bf16[4,1,128,2,576]{2,4,3,1,0:T(8,128)(2,1)S(1)} async-done(((bf16[4,1,128,2,576]{2,4,3,1,0:T(8,128)(2,1)}), bf16[4,1,128,2,576]{2,4,3,1,0:T(8,128)(2,1)S(1)}, u32[]{:S(2)}, u32[]{:S(2)}) %all-to-all-start.6) | async-done | bytes 1179680 | tf_op jit(solution)/shard_map/all_to_all | solution.py:25
  391.8 0.7 fusion.29
  392.5 2.2 fusion.46
  394.8 4.7 all_to_all.63
  399.6 1.7 fusion.19
  401.4 46.4 %all_to_all.64 = f32[32,16,128]{2,1,0:T(8,128)S(1)} all-to-all(f32[32,16,128]{2,1,0:T(8,128)S(1)} %broadcast_in_dim.83), channel_id=1, replica_groups=mesh['parts'=2,'step'=32,'frame'=4,'head'=2] {'step'}, dimensions={0} | all-to-all | bytes 524288 | tf_op jit(solution)/shard_map/all_to_all | solution.py:25
  448.4 1.3 fusion.15
  449.7 1.2 broadcast_in_dim.85
  450.9 5.0 all-to-all-start.9
  455.9 14.6 %all-to-all-done.9 = bf16[4,1,128,2,576]{2,4,3,1,0:T(8,128)(2,1)S(1)} async-done(((bf16[4,1,128,2,576]{2,4,3,1,0:T(8,128)(2,1)}), bf16[4,1,128,2,576]{2,4,3,1,0:T(8,128)(2,1)S(1)}, u32[]{:S(2)}, u32[]{:S(2)}) %all-to-all-start.9) | async-done | bytes 1179680 | tf_op jit(solution)/shard_map/all_to_all | solution.py:25
  471.9 0.7 fusion.31
  472.6 2.2 fusion.44
  474.9 4.7 all_to_all.65
  479.8 1.4 fusion.17
  481.3 46.4 %all_to_all.66 = f32[32,16,128]{2,1,0:T(8,128)S(1)} all-to-all(f32[32,16,128]{2,1,0:T(8,128)S(1)} %broadcast_in_dim.88), channel_id=1, replica_groups=mesh['parts'=2,'step'=32,'frame'=4,'head'=2] {'step'}, dimensions={0} | all-to-all | bytes 524288 | tf_op jit(solution)/shard_map/all_to_all | solution.py:25
  527.8 1.3 fusion.77
  529.1 2.6 pad_maximum_fusion
  531.7 53.0 %psum.14 = f32[4]{0:T(128)S(1)} all-reduce(f32[4]{0:T(128)S(1)} %pad_maximum_fusion), channel_id=1, replica_groups=mesh['parts'=2,'step'=32,'frame'=4,'head'=2] {'step'}, use_global_device_ids=true, to_apply=%region_22.23 | all-reduce | flops 4 | bytes 32 | tf_op jit(solution)/shard_map/psum | solution.py:68
  584.7 9.2 %psum.15 = f32[4]{0:T(128)S(1)} all-reduce(f32[4]{0:T(128)S(1)} %psum.14), channel_id=1, replica_groups=mesh['parts'=2,'step'=32,'frame'=4,'head'=2] {'frame'}, use_global_device_ids=true, to_apply=%region_23.24 | all-reduce | flops 4 | bytes 32 | tf_op jit(solution)/shard_map/psum | solution.py:68
  (112 shorter events, 11.2 us)
Async XLA Ops:
  7.2 3.5 copy-start
  7.2 173.0 %all-gather.3.cloned.1.call-start = ((), (), s32[]{:S(2)}) async-start(), calls=%async_computation.12 | async-start | bytes 6082560 | tf_op jit(solution)/shard_map/all_gather | solution.py:15
  192.4 6.5 %copy-start.12 = (f32[1152]{0:T(1024)S(1)}, f32[1152]{0:T(1024)}, u32[]{:S(2)}) copy-start(f32[1152]{0:T(1024)} %param.20) | copy-start | bytes 13828
  202.3 7.8 %copy-start.5 = (bf16[1,128,3,576]{1,3,2,0:T(8,128)(2,1)}, bf16[1,128,3,576]{1,3,2,0:T(8,128)(2,1)S(1)}, u32[]{:S(2)}) copy-start(bf16[1,128,3,576]{1,3,2,0:T(8,128)(2,1)S(1)} %fusion.12) | copy-start | bytes 1327108
  202.3 6.5 %copy-start.13 = (f32[128]{0:T(128)S(1)}, f32[128]{0:T(128)}, u32[]{:S(2)}) copy-start(f32[128]{0:T(128)} %param.17) | copy-start | bytes 1540
  202.3 7.1 %copy-start.14 = (f32[128]{0:T(128)S(1)}, f32[128]{0:T(128)}, u32[]{:S(2)}) copy-start(f32[128]{0:T(128)} %param.18) | copy-start | bytes 1540
  203.6 14.8 %all-to-all-start = ((bf16[4,1,128,2,576]{2,4,3,1,0:T(8,128)(2,1)}), bf16[4,1,128,2,576]{2,4,3,1,0:T(8,128)(2,1)S(1)}, u32[]{:S(2)}, u32[]{:S(2)}) async-start(bf16[4,1,128,2,576]{2,4,3,1,0:T(8,128)(2,1)} %broadcast_in_dim.69), calls=%async_computation | async-start | bytes 2359296 | tf_op jit(solution)/shard_map/all_to_all | solution.py:25
  210.1 8.5 %slice-start = ((bf16[1,128,3,576]{1,3,2,0:T(8,128)(2,1)}), bf16[1,128,1,576]{1,3,2,0:T(8,128)(2,1)S(1)}, s32[]{:S(2)}) async-start(bf16[1,128,3,576]{1,3,2,0:T(8,128)(2,1)} %copy-done.5), calls=%async_computation.13 | async-start | bytes 294912 | tf_op jit(solution)/shard_map/slice | solution.py:123
  222.7 4.8 copy-start.10
  222.7 4.8 copy-start.11
  227.6 57.6 %copy-start.4 = (bf16[128,1152]{1,0:T(8,128)(2,1)S(1)}, bf16[128,1152]{1,0:T(8,128)(2,1)}, u32[]{:S(2)}) copy-start(bf16[128,1152]{1,0:T(8,128)(2,1)} %param.13) | copy-start | bytes 884740
  227.6 57.6 %copy-start.9 = (bf16[16,1152]{1,0:T(8,128)(2,1)S(1)}, bf16[16,1152]{1,0:T(8,128)(2,1)}, u32[]{:S(2)}) copy-start(bf16[16,1152]{1,0:T(8,128)(2,1)} %param.19) | copy-start | bytes 110596
  229.9 55.1 %all-to-all-start.2 = ((f32[32,16,128]{2,1,0:T(8,128)}), f32[32,16,128]{2,1,0:T(8,128)S(1)}, u32[]{:S(2)}, u32[]{:S(2)}) async-start(f32[32,16,128]{2,1,0:T(8,128)} %broadcast_in_dim.72), calls=%async_computation.2 | async-start | bytes 524288 | tf_op jit(solution)/shard_map/all_to_all | solution.py:25
  289.0 6.2 %copy-start.7 = (bf16[1,128,3,576]{1,3,2,0:T(8,128)(2,1)}, bf16[1,128,3,576]{1,3,2,0:T(8,128)(2,1)S(1)}, u32[]{:S(2)}) copy-start(bf16[1,128,3,576]{1,3,2,0:T(8,128)(2,1)S(1)} %fusion.13) | copy-start | bytes 1327108
  290.2 19.5 %all-to-all-start.3 = ((bf16[4,1,128,2,576]{2,4,3,1,0:T(8,128)(2,1)}), bf16[4,1,128,2,576]{2,4,3,1,0:T(8,128)(2,1)S(1)}, u32[]{:S(2)}, u32[]{:S(2)}) async-start(bf16[4,1,128,2,576]{2,4,3,1,0:T(8,128)(2,1)} %broadcast_in_dim.75), calls=%async_computation.3 | async-start | bytes 2359296 | tf_op jit(solution)/shard_map/all_to_all | solution.py:25
  295.2 14.8 %slice-start.2 = ((bf16[1,128,3,576]{1,3,2,0:T(8,128)(2,1)}), bf16[1,128,1,576]{1,3,2,0:T(8,128)(2,1)S(1)}, s32[]{:S(2)}) async-start(bf16[1,128,3,576]{1,3,2,0:T(8,128)(2,1)} %copy-done.7), calls=%async_computation.15 | async-start | bytes 294912 | tf_op jit(solution)/shard_map/slice | solution.py:123
  319.0 48.9 %copy-start.2 = (bf16[1152,1728]{0,1:T(8,128)(2,1)S(1)}, bf16[1152,1728]{0,1:T(8,128)(2,1)}, u32[]{:S(2)}) copy-start(bf16[1152,1728]{0,1:T(8,128)(2,1)} %copy.26) | copy-start | bytes 11943940
  369.1 6.2 %copy-start.8 = (bf16[1,128,3,576]{1,3,2,0:T(8,128)(2,1)}, bf16[1,128,3,576]{1,3,2,0:T(8,128)(2,1)S(1)}, u32[]{:S(2)}) copy-start(bf16[1,128,3,576]{1,3,2,0:T(8,128)(2,1)S(1)} %fusion.14) | copy-start | bytes 1327108
  370.4 20.0 %all-to-all-start.6 = ((bf16[4,1,128,2,576]{2,4,3,1,0:T(8,128)(2,1)}), bf16[4,1,128,2,576]{2,4,3,1,0:T(8,128)(2,1)S(1)}, u32[]{:S(2)}, u32[]{:S(2)}) async-start(bf16[4,1,128,2,576]{2,4,3,1,0:T(8,128)(2,1)} %broadcast_in_dim.80), calls=%async_computation.6 | async-start | bytes 2359296 | tf_op jit(solution)/shard_map/all_to_all | solution.py:25
  375.3 15.3 %slice-start.3 = ((bf16[1,128,3,576]{1,3,2,0:T(8,128)(2,1)}), bf16[1,128,1,576]{1,3,2,0:T(8,128)(2,1)S(1)}, s32[]{:S(2)}) async-start(bf16[1,128,3,576]{1,3,2,0:T(8,128)(2,1)} %copy-done.8), calls=%async_computation.16 | async-start | bytes 294912 | tf_op jit(solution)/shard_map/slice | solution.py:123
  399.6 48.8 %copy-start.3 = (bf16[1152,1728]{0,1:T(8,128)(2,1)S(1)}, bf16[1152,1728]{0,1:T(8,128)(2,1)}, u32[]{:S(2)}) copy-start(bf16[1152,1728]{0,1:T(8,128)(2,1)} %copy.26) | copy-start | bytes 11943940
  449.7 6.2 %copy-start.6 = (bf16[1,128,3,576]{1,3,2,0:T(8,128)(2,1)}, bf16[1,128,3,576]{1,3,2,0:T(8,128)(2,1)S(1)}, u32[]{:S(2)}) copy-start(bf16[1,128,3,576]{1,3,2,0:T(8,128)(2,1)S(1)} %fusion.15) | copy-start | bytes 1327108
  450.9 19.6 %all-to-all-start.9 = ((bf16[4,1,128,2,576]{2,4,3,1,0:T(8,128)(2,1)}), bf16[4,1,128,2,576]{2,4,3,1,0:T(8,128)(2,1)S(1)}, u32[]{:S(2)}, u32[]{:S(2)}) async-start(bf16[4,1,128,2,576]{2,4,3,1,0:T(8,128)(2,1)} %broadcast_in_dim.85), calls=%async_computation.9 | async-start | bytes 2359296 | tf_op jit(solution)/shard_map/all_to_all | solution.py:25
  455.9 14.9 %slice-start.1 = ((bf16[1,128,3,576]{1,3,2,0:T(8,128)(2,1)}), bf16[1,128,1,576]{1,3,2,0:T(8,128)(2,1)S(1)}, s32[]{:S(2)}) async-start(bf16[1,128,3,576]{1,3,2,0:T(8,128)(2,1)} %copy-done.6), calls=%async_computation.14 | async-start | bytes 294912 | tf_op jit(solution)/shard_map/slice | solution.py:123
  479.6 114.8 %copy-start.1 = (bf16[128,1152]{1,0:T(8,128)(2,1)S(1)}, bf16[128,1152]{1,0:T(8,128)(2,1)}, u32[]{:S(2)}) copy-start(bf16[128,1152]{1,0:T(8,128)(2,1)} %param.14) | copy-start | bytes 884740
Sparse Core Ops, SparseCore 0:
  10.2 169.9 all-gather.2
where the time goes:
time: 603 us; the launch traced here: 601 us
  waiting for transfers between devices  263 us (44%)
  blocking collectives  220 us (36%)
  starting transfers between devices  32.5 us (5%)
  matrix products  32.2 us (5%)
  local copies, waits for them, and re-layouts  27 us (4%)
  between operations  16.1 us (3%)
  other arithmetic  10.7 us (2%)
    all_gather x1, waiting for transfers between devices, in_one_piece(): result, at, outs = (lax.all_gather(both, axis, axis=dim, tiled=True), 0, [])  168 us
    all_to_all x7, blocking collectives, sent_to_all(): lax.all_to_all(jnp.broadcast_to(value[None], (count, *value.shape)), axis...  158 us
    all_to_all x5, waiting for transfers between devices, sent_to_all(): lax.all_to_all(jnp.broadcast_to(value[None], (count, *value.shape)), axis...  94.6 us
    psum x2, blocking collectives, over_axes(): value = lax.psum(value, axis)  62.2 us
    all_to_all x5, starting transfers between devices, sent_to_all(): lax.all_to_all(jnp.broadcast_to(value[None], (count, *value.shape)), axis...  32.4 us
  transfers between devices with their start and end apart: 6, of which 6 were waited for; matrix products, arithmetic and copies ran while one was open for 0% of the time, Pallas kernels for 0%

commit v1 on v0

v1 whole, which is shorter than its diff:
```python
import functools
import math

import jax
import jax.numpy as jnp
from jax import lax
from jax.experimental import pallas as pl
from jax.experimental.pallas import tpu as pltpu
from jax.sharding import Mesh
from jax.sharding import PartitionSpec as P

HDIM = 72
ITERS = 4
ZLO = 4
F32 = jnp.float32
BF16 = jnp.bfloat16
STEP = ("zhi", "zlo")
HOOD = ("frame", "zlo", "head")


def three_parts(a):
    hi = lax.reduce_precision(a, 8, 7)
    mid = lax.reduce_precision(a - hi, 8, 7)
    return hi.astype(BF16), mid.astype(BF16), (a - hi - mid).astype(BF16)


def chosen(pieces, index):
    out = pieces[0]
    for at, piece in enumerate(pieces[1:], 1):
        out = jnp.where(index == at, piece, out)
    return out


def vmem_call(body, out_shape, *args, scratch=(), flops=0, name=None):
    spec = pl.BlockSpec(memory_space=pltpu.VMEM)
    return pl.pallas_call(
        body,
        out_shape=out_shape,
        in_specs=[spec] * len(args),
        out_specs=jax.tree.map(lambda _: spec, out_shape),
        scratch_shapes=list(scratch),
        cost_estimate=pl.CostEstimate(flops=flops, bytes_accessed=0, transcendentals=0),
        name=name,
    )(*args)


def eps_body(heads, steps, lat, x_ref, bext_ref, a_ref, c_ref, wfp_ref, out_ref, xs, es):
    cols = heads * HDIM
    tokens = x_ref.shape[0]
    width = bext_ref.shape[0] - lat - 3 * cols
    assert width == 0
    model = 1.0 / c_ref.shape[1]
    xs[...] = x_ref[...].astype(F32).T
    scale = math.log2(math.e) / math.sqrt(HDIM)
    ones16 = jnp.ones((lat, tokens), F32)
    ones8 = jnp.ones((8, tokens), F32)

    def one_step(step, carry):
        rows = pl.ds(pl.multiple_of(step * lat, lat), lat)
        x = xs[rows, :]
        xcat = jnp.concatenate([x, x, x, ones16], axis=0).astype(BF16)
        mixed = jnp.dot(a_ref[step], xcat, preferred_element_type=F32) + bext_ref[...]
        quad = mixed[3 * cols :, :]
        square = jnp.sum(x * quad, axis=0, keepdims=True) + c_ref[pl.ds(step, 1), :]
        rate = lax.rsqrt(jnp.maximum(square, 0.0) + 1e-06)
        outs = []
        for head in range(heads):
            q = mixed[head * HDIM : (head + 1) * HDIM, :]
            k = mixed[cols + head * HDIM : cols + (head + 1) * HDIM, :]
            v = mixed[2 * cols + head * HDIM : 2 * cols + (head + 1) * HDIM, :]
            q = (q * (rate * scale)).astype(BF16)
            k = (k * rate).astype(BF16)
            v = jnp.concatenate([v * rate, ones8], axis=0).astype(BF16)
            s = lax.dot_general(k, q, (((0,), (0,)), ((), ())), preferred_element_type=F32)
            top = jnp.max(s, axis=0, keepdims=True)
            e = jnp.exp2(s - top).astype(BF16)
            o = jnp.dot(v, e, preferred_element_type=F32)
            outs.append(o[:HDIM, :] * (1.0 / o[HDIM : HDIM + 1, :]))
        o = jnp.concatenate(outs, axis=0).astype(BF16)
        part = jnp.dot(wfp_ref[...], o, preferred_element_type=F32)
        es[rows, :] = part[:lat, :] + part[lat:, :]
        return carry

    lax.fori_loop(0, steps, one_step, 0)
    out_ref[...] = es[...].T.astype(BF16)


def eps_part(x, bext, a_all, c_all, wfp, lat):
    steps = a_all.shape[0]
    tokens = x.shape[0]
    heads = wfp.shape[1] // HDIM
    flops = 2 * steps * tokens * (bext.shape[0] * 64 + heads * tokens * 160)
    return vmem_call(
        functools.partial(eps_body, heads, steps, lat),
        jax.ShapeDtypeStruct((tokens, steps * lat), BF16),
        x,
        bext,
        a_all,
        c_all,
        wfp,
        scratch=(
            pltpu.VMEM((steps * lat, tokens), F32),
            pltpu.VMEM((steps * lat, tokens), F32),
        ),
        flops=flops,
        name="eps_part",
    )


def advance(lat, frames, cores, got_ref, x_ref, noise_ref, base_ref, fblk_ref, coef_ref):
    groups, rows, lanes = x_ref.shape
    lane = lax.broadcasted_iota(jnp.int32, (rows, lanes), 1)
    before = jnp.zeros((rows, lanes), F32)
    drifts, states = [], []
    square = jnp.zeros((rows, lanes), F32)
    for group in range(groups):
        old = x_ref[group]
        total = base_ref[group]
        for frame in range(frames):
            for core in range(cores):
                member = (frame * groups + group) * cores + core
                total = total + got_ref[member].astype(F32)
        xb = old.astype(BF16)
        total = total + jnp.dot(
            jnp.concatenate([xb, xb, xb], axis=1), fblk_ref[...], preferred_element_type=F32
        )
        drift = (
            coef_ref[pl.ds(group, 1), :] * old + coef_ref[pl.ds(groups + group, 1), :] * total
        )
        running = drift
        shift = lat
        while shift < lanes:
            running = running + jnp.where(lane >= shift, pltpu.roll(running, shift, 1), 0.0)
            shift *= 2
        own = jnp.where(lane >= lat, pltpu.roll(running, lat, 1), 0.0)
        new = noise_ref[...] + before + own
        last = jnp.where(lane >= lanes - lat, running, 0.0)
        shift = lanes // 2
        while shift >= lat:
            last = last + pltpu.roll(last, shift, 1)
            shift //= 2
        before = before + last
        change = new - old
        square = square + change * change
        drifts.append(drift)
        states.append(new)
    return drifts, states, square


def glue_body(lat, frames, cores, got_ref, x_ref, noise_ref, base_ref, fblk_ref, coef_ref,
              new_ref, send_ref, square_ref):
    _, states, square = advance(
        lat, frames, cores, got_ref, x_ref, noise_ref, base_ref, fblk_ref, coef_ref
    )
    square_ref[...] = square
    groups = len(states)
    for group, new in enumerate(states):
        new_ref[group] = new
        rounded = new.astype(BF16)
        for frame in range(frames):
            for core in range(cores):
                send_ref[(frame * groups + group) * cores + core] = rounded


def last_body(lat, frames, cores, where_ref, got_ref, x_ref, noise_ref, base_ref, fblk_ref,
              coef_ref, sq0_ref, sq1_ref, sq2_ref, send_ref):
    drifts, states, square = advance(
        lat, frames, cores, got_ref, x_ref, noise_ref, base_ref, fblk_ref, coef_ref
    )
    groups, rows, lanes = x_ref.shape
    half = rows // 2
    zhi = where_ref[0]
    width = groups * lat
    first = zhi * groups
    per_group = lanes // lat
    picked = chosen([s + d for s, d in zip(states, drifts)], first // per_group)
    offset = lax.rem(first, per_group) * lat
    lane = lax.broadcasted_iota(jnp.int32, (half, lanes), 1)
    turn = lax.rem(lanes - offset, lanes)
    top = pltpu.roll(picked[:half], turn, 1)
    bottom = pltpu.roll(picked[half:], lax.rem(turn + width, lanes), 1)
    piece = jnp.where(lane < width, top, bottom)
    sums = jnp.zeros((half, lanes), F32)
    inner = lax.rem(lane, lat)
    for at, sq in enumerate((sq0_ref[...], sq1_ref[...], sq2_ref[...], square)):
        sums = jnp.where(inner == at, jnp.sum(sq), sums)
    for group in range(groups):
        slot = (group + 1) % groups
        mixed = jnp.where(lane // lat == slot, sums, piece)
        for frame in range(frames):
            for core in range(cores):
                send_ref[(frame * groups + group) * cores + core] = mixed


def end_body(lat, frames, cores, cells, where_ref, got_ref, traj_ref, norm_ref):
    members, half, lanes = got_ref.shape
    groups = members // (frames * cores)
    frame, zlo = where_ref[1], where_ref[2]
    width = groups * lat
    everyone = got_ref[0]
    for member in range(1, members):
        everyone = everyone + got_ref[member]
    slot = lax.rem(zlo + 1, groups)
    sums = pltpu.roll(everyone, lax.rem(lanes - slot * lat, lanes), 1)
    norm_ref[...] = jnp.sqrt(sums / cells + 1e-06)
    rows = []
    back = lax.rem(lanes - zlo * lat, lanes)
    for own in range(groups * cores):
        piece = got_ref[frame * (groups * cores) + own]
        rows.append(pltpu.roll(piece, back, 1))
        rows.append(pltpu.roll(piece, lax.rem(back + lanes - width, lanes), 1))
    traj_ref[...] = jnp.concatenate(rows, axis=0).T[:lat, :]


def smem_first(body, out_shape, where, *args, name=None):
    spec = pl.BlockSpec(memory_space=pltpu.VMEM)
    return pl.pallas_call(
        body,
        out_shape=out_shape,
        in_specs=[pl.BlockSpec(memory_space=pltpu.SMEM)] + [spec] * len(args),
        out_specs=jax.tree.map(lambda _: spec, out_shape),
        name=name,
    )(where, *args)


def local(
    start_noise,
    position,
    time_table,
    time_index,
    sched_index,
    coef_keep,
    coef_noise,
    w_in,
    norm_gain,
    w_qkv,
    w_proj,
    w_final,
):
    lat, row_count = start_noise.shape
    rows_d = w_qkv.shape[0]
    model = position.shape[1]
    frames, cores = lax.axis_size("frame"), lax.axis_size("head")
    zlo_n, zhi_n = lax.axis_size("zlo"), lax.axis_size("zhi")
    step_n = zlo_n * zhi_n
    steps = step_n // zlo_n
    tokens = row_count * frames
    cols = w_qkv.shape[2] // frames
    heads = cols // HDIM
    members = frames * zlo_n * cores
    mine = tokens // members
    lanes = steps * lat
    frame, zlo, zhi, core = (lax.axis_index(a) for a in ("frame", "zlo", "zhi", "head"))
    step = zhi * zlo_n + zlo

    proj_mine = chosen([w_proj[:, f * cols : (f + 1) * cols] for f in range(frames)], frame)
    final_mine = lax.dynamic_slice_in_dim(w_final, step * rows_d, rows_d, 1)
    mix = jnp.dot(final_mine, proj_mine, preferred_element_type=F32)
    mix = lax.all_to_all(mix.reshape(zlo_n, lat // zlo_n, cols), "zlo", 0, 0, tiled=True)
    mix = jnp.sum(mix, axis=0).T.astype(BF16)

    qkv_mine = chosen([w_qkv[:, :, f * cols : (f + 1) * cols] for f in range(frames)], frame)
    main = [qkv_mine[:, k, :lanes] for k in range(3)]
    rest = jnp.concatenate([qkv_mine[:, k, lanes:] for k in range(3)], axis=1)
    tall = rows_d // 2
    pieces = cols // tall
    side = jnp.concatenate(
        [rest[:tall], rest[tall:]] + [mix[g * tall : (g + 1) * tall] for g in range(pieces)], axis=1
    )
    index_row = jnp.concatenate([time_index, sched_index]).astype(BF16)
    index_row = jnp.pad(index_row, (0, lanes - 2))[None]
    payload = jnp.concatenate(main + [side, index_row], axis=0)
    gathered = lax.all_gather(payload, STEP, axis=0)

    noise_rows = jnp.pad(start_noise.astype(BF16), ((0, 0), (0, model - row_count)))
    frame_load = jnp.concatenate([position, noise_rows], axis=0)
    frame_all = lax.all_to_all(
        jnp.broadcast_to(frame_load[None], (frames, *frame_load.shape)), "frame", 0, 0, tiled=True
    )
    positions = frame_all[:, :row_count].reshape(tokens, model)
    noise_all = frame_all[:, row_count:, :row_count]

    w_main = [
        gathered[:, k * rows_d : (k + 1) * rows_d].reshape(step_n * rows_d, lanes) for k in range(3)
    ]
    sides = gathered[:, 3 * rows_d : 3 * rows_d + tall]
    extra = cols - lanes
    w_rest = jnp.concatenate([sides[:, :, : 3 * extra], sides[:, :, 3 * extra : 6 * extra]], axis=1)
    w_rest = w_rest.reshape(step_n * rows_d, 3 * extra)
    part = lat // zlo_n
    mixes = sides[:, :, 6 * extra :].astype(F32).reshape(zhi_n, zlo_n, tall, pieces, part)
    mixes = jnp.sum(mixes, axis=0).transpose(0, 3, 2, 1).reshape(lat, cols)
    mix_hi = lax.reduce_precision(mixes, 8, 7)
    wfp = jnp.concatenate([mix_hi, mixes - mix_hi], axis=0).astype(BF16)
    table_rows = time_table.shape[0]
    indices = gathered[:, 3 * rows_d + tall, :2].astype(F32)
    spots = jnp.arange(table_rows, dtype=F32)
    pick_time = (indices[:, :1] == spots[None]).astype(BF16)
    pick_sched = (indices[:, 1:] == spots[None]).astype(F32)
    temb_all = jnp.dot(pick_time, time_table, preferred_element_type=F32).astype(BF16)
    keep = jnp.sum(pick_sched * coef_keep[None], axis=1)
    rate = jnp.sum(pick_sched * coef_noise[None], axis=1)
    coef = jnp.repeat(jnp.concatenate([keep, rate]).reshape(2 * zlo_n, steps), lat, axis=1)
    temb = lax.dynamic_slice_in_dim(temb_all, zlo * steps, steps, 0)

    every = jnp.concatenate([positions, w_in, temb], axis=0)
    scaled = every.astype(F32) * norm_gain[None]
    scaled_hi = lax.reduce_precision(scaled, 8, 7)
    scaled_lo = (scaled - scaled_hi).astype(BF16)
    scaled_hi = scaled_hi.astype(BF16)

    def against(w):
        dims = (((0,), (1,)), ((), ()))
        return lax.dot_general(w, scaled_hi, dims, preferred_element_type=F32) + lax.dot_general(
            w, scaled_lo, dims, preferred_element_type=F32
        )

    thin = against(w_rest)
    blocks = []
    for k in range(3):
        blocks += [against(w_main[k]), thin[k * extra : (k + 1) * extra]]
    gram = lax.dot_general(
        jnp.concatenate([w_in, temb], axis=0),
        every,
        (((1,), (1,)), ((), ())),
        preferred_element_type=F32,
    )
    inv = 1.0 / model
    linear = jnp.concatenate(
        blocks + [gram[:lat] * jnp.where(jnp.arange(every.shape[0]) // lat == tokens // lat, inv, 2 * inv)],
        axis=0,
    )
    bext = linear[:, :tokens]
    latent = linear[:, tokens : tokens + lat]
    time_part = linear[:, tokens + lat :]
    latent_parts = jnp.concatenate(three_parts(latent), axis=1)
    time_parts = jnp.stack(three_parts(time_part.T), axis=2)
    a_all = jnp.concatenate(
        [
            jnp.broadcast_to(latent_parts[None], (steps, *latent_parts.shape)),
            jnp.pad(time_parts, ((0, 0), (0, 0), (0, lat - 3))),
        ],
        axis=2,
    )
    wide = positions.astype(F32)
    temb_wide = temb.astype(F32)
    c_all = (
        jnp.sum(wide * wide, axis=1)[None]
        + 2.0 * gram[lat:, :tokens]
        + jnp.sum(temb_wide * temb_wide, axis=1)[:, None]
    ) * inv

    at = (zlo * cores + core) * mine
    own_position = lax.dynamic_slice_in_dim(position, at, mine, 0)
    own_noise = lax.dynamic_slice_in_dim(start_noise, at, mine, 1).T
    nt = (((1,), (1,)), ((), ()))
    base_own = lax.dot_general(own_position, w_final, nt, preferred_element_type=F32)
    base_time = lax.dot_general(temb_all, w_final, nt, preferred_element_type=F32)
    base = jnp.tile(base_own, (1, steps))[None] + base_time.reshape(zlo_n, 1, lanes)
    final_in = lax.dot_general(w_in, w_final, nt, preferred_element_type=F32)
    fblk = jnp.concatenate(
        [jnp.kron(jnp.eye(steps, dtype=F32), p.astype(F32)) for p in three_parts(final_in)], axis=0
    ).astype(BF16)
    noise = jnp.tile(own_noise, (1, steps))
    states = jnp.broadcast_to(noise[None], (zlo_n, mine, lanes))
    x = jnp.tile(noise_all.transpose(0, 2, 1).reshape(tokens, lat), (1, steps))

    squares = []
    where = jnp.stack([zhi, frame, zlo]).astype(jnp.int32)
    for iteration in range(ITERS):
        part_eps = eps_part(x, bext, a_all, c_all, wfp, lat)
        got = lax.all_to_all(part_eps.reshape(members, mine, lanes), HOOD, 0, 0, tiled=True)
        if iteration < ITERS - 1:
            states, send, square = vmem_call(
                functools.partial(glue_body, lat, frames, cores),
                (
                    jax.ShapeDtypeStruct(states.shape, F32),
                    jax.ShapeDtypeStruct((members, mine, lanes), BF16),
                    jax.ShapeDtypeStruct((mine, lanes), F32),
                ),
                got,
                states,
                noise,
                base,
                fblk,
                coef,
                name="advance",
            )
            squares.append(square)
            x = lax.all_to_all(send, HOOD, 0, 0, tiled=True).reshape(tokens, lanes)
        else:
            send = smem_first(
                functools.partial(last_body, lat, frames, cores),
                jax.ShapeDtypeStruct((members, mine // 2, lanes), F32),
                where,
                got,
                states,
                noise,
                base,
                fblk,
                coef,
                *squares,
                name="last",
            )
    ended = lax.all_to_all(send, HOOD, 0, 0, tiled=True)
    trajectory, norms = smem_first(
        functools.partial(end_body, lat, frames, cores, float(step_n * lat * tokens)),
        (
            jax.ShapeDtypeStruct((lat, row_count), F32),
            jax.ShapeDtypeStruct((mine // 2, lanes), F32),
        ),
        where,
        ended,
        name="end",
    )
    return trajectory[None], norms[0, :ITERS]


def solution(mesh):
    names = ("parts", "zhi", "zlo", "frame", "head")
    sizes = mesh.shape
    devices = mesh.devices.reshape(
        sizes["parts"], sizes["step"] // ZLO, ZLO, sizes["frame"], sizes["head"]
    )
    return jax.shard_map(
        local,
        mesh=Mesh(devices, names),
        in_specs=(
            P("parts", "frame"),
            P("frame", None),
            P(),
            P(STEP),
            P(STEP),
            P(),
            P(),
            P(),
            P(),
            P(STEP, None, "head"),
            P(STEP, "head"),
            P(),
        ),
        out_specs=(P(STEP, "parts", "frame"), P("parts")),
        check_vma=False,
    )
```

time: 603 us -> 338 us (0.56)
  the two profiles are of different devices: /device:TPU:34 before, /device:TPU:33 now
where the time goes in v1:
time: 338 us; the launch traced here: 336 us
  blocking collectives  166 us (49%)
  Pallas kernels  71.6 us (21%)
  starting transfers between devices  36.5 us (11%)
  local copies, waits for them, and re-layouts  21.4 us (6%)
  waiting for transfers between devices  14.6 us (4%)
  matrix products  13.4 us (4%)
  other arithmetic  9.34 us (3%)
    all_gather x1, blocking collectives, local(): gathered = lax.all_gather(payload, STEP, axis=0)  84.4 us
    pallas_call x7, Pallas kernels, vmem_call(): pl.pallas_call(body, out_shape=out_shape, in_specs=[spec] * len(args), ou...  67.5 us
    all_to_all x3, blocking collectives, local(): x = lax.all_to_all(send, HOOD, 0, 0, tiled=True).reshape(tokens, lanes)  41 us
    all_to_all x2, blocking collectives, local(): lax.all_to_all(part_eps.reshape(members, mine, lanes), HOOD, 0, 0, tiled=...  27.3 us
    all_to_all x2, starting transfers between devices, local(): lax.all_to_all(part_eps.reshape(members, mine, lanes), HOOD, 0, 0, tiled=...  23.2 us
    all_to_all x2, waiting for transfers between devices, local(): lax.all_to_all(part_eps.reshape(members, mine, lanes), HOOD, 0, 0, tiled=...  14.6 us
    all_to_all x1, blocking collectives, local(): ended = lax.all_to_all(send, HOOD, 0, 0, tiled=True)  13.7 us
    all_to_all x1, starting transfers between devices, local(): lax.all_to_all(mix.reshape(zlo_n, lat // zlo_n, cols), 'zlo', 0, 0, tiled...  9.02 us
  transfers between devices with their start and end apart: 4, of which 2 were waited for; matrix products, arithmetic and copies ran while one was open for 5% of the time, Pallas kernels for 0%

profile of v1, /device:TPU:33, one launch (start us, length us, event | category | flops | bytes accessed | tf_op | source)
XLA Modules:
  0.0 335.8 jit_solution(13328850512563064296)
XLA Ops:
  0.7 1.1 fusion.18
  2.4 9.0 %all-to-all-start.1 = ((f32[4,4,144]{2,1,0:T(4,128)}), f32[4,4,144]{2,1,0:T(4,128)S(1)}, u32[]{:S(2)}, u32[]{:S(2)}) async-start(f32[4,4,144]{2,1,0:T(4,128)} %reshape.130), calls=%async_computation.1 | async-start | bytes 32768 | tf_op jit(solution)/shard_map/all_to_all | solution.py:259
  11.4 1.2 select_select_fusion
  14.6 0.8 dynamic-slice_bitcast_fusion
  15.4 0.9 fusion.16
  16.3 0.9 fusion.38
  17.3 1.0 fusion.8
  18.9 0.8 mul.148
  19.7 0.8 mul.145
  20.5 0.8 mul.142
  21.3 1.2 broadcast_in_dim.28
  22.5 4.3 %all-to-all-start = ((bf16[4,144,1152]{2,1,0:T(8,128)(2,1)}), bf16[4,144,1152]{2,1,0:T(8,128)(2,1)S(1)}, u32[]{:S(2)}, u32[]{:S(2)}) async-start(bf16[4,144,1152]{2,1,0:T(8,128)(2,1)} %broadcast_in_dim.28), calls=%async_computation | async-start | bytes 2654208 | tf_op jit(solution)/shard_map/all_to_all | solution.py:277
  28.2 84.4 %all-gather.1 = bf16[32,127,128]{2,1,0:T(8,128)(2,1)S(1)} all-gather(bf16[1,127,128]{2,1,0:T(8,128)(2,1)S(1)} %bitcast.99), channel_id=2, replica_groups=mesh['parts'=2,'zhi'=8,'zlo'=4,'frame'=4,'head'=2] {'zhi','zlo'}, dimensions={0}, use_global_device_ids=true | all-gather | bytes 1072896 | tf_op jit(solution)/shard_map/all_gather | solution.py:273
  114.0 0.8 reshape.154
  118.2 1.1 fusion.11
  119.8 1.2 convolution_add_fusion.3
  121.6 1.2 convolution_add_fusion
  122.8 1.1 copy.191
  123.9 1.6 fusion.5
  125.5 1.2 convolution_add_fusion.1
  126.8 1.1 copy.190
  127.9 1.6 fusion.7
  129.5 1.2 convolution_add_fusion.2
  130.8 1.1 copy.189
  132.0 0.8 slice_dynamic-update-slice_fusion.2
  133.1 1.1 slice.208.bext_ref
  136.0 1.4 fusion.32.c_ref
  137.6 1.5 fusion.2.a_ref
  139.1 15.2 %eps_part.4 = bf16[512,128]{1,0:T(8,128)(2,1)} custom-call(bf16[512,128]{1,0:T(8,128)(2,1)} %copy.198.x_ref, f32[448,512]{1,0:T(8,128)} %slice.208.bext_ref, bf16[8,448,64]{2,1,0:T(8,128)(2,1)} %fusion.2.a_ref, f32[8,512]{1,0:T(8,128)} %fusion.32.c_ref, bf16[32,144]{1,0:T(8,128)(2,1)} %pad_maximum_fusion.4.wfp_ref), custom_call_target="tpu_custom_call" | custom-call | flops 1577058304 | tf_op jit(solution)/shard_map/eps_part/pallas_call | solution.py:36
  154.4 19.0 %all-to-all-start.2 = ((bf16[32,16,128]{2,1,0:T(8,128)(2,1)}), bf16[32,16,128]{2,1,0:T(8,128)(2,1)S(1)}, u32[]{:S(2)}, u32[]{:S(2)}) async-start(bf16[32,16,128]{2,1,0:T(8,128)(2,1)} %bitcast.100), calls=%async_computation.2 | async-start | bytes 262144 | tf_op jit(solution)/shard_map/all_to_all | solution.py:372
  175.5 6.5 %all-to-all-done.2.got_ref = bf16[32,16,128]{2,1,0:T(8,128)(2,1)S(1)} async-done(((bf16[32,16,128]{2,1,0:T(8,128)(2,1)}), bf16[32,16,128]{2,1,0:T(8,128)(2,1)S(1)}, u32[]{:S(2)}, u32[]{:S(2)}) %all-to-all-start.2) | async-done | bytes 131104 | tf_op jit(solution)/shard_map/all_to_all | solution.py:372
  182.6 2.3 advance.3
  184.9 13.7 %all_to_all.50 = bf16[32,16,128]{2,1,0:T(8,128)(2,1)} all-to-all(bf16[32,16,128]{2,1,0:T(8,128)(2,1)} %get-tuple-element.13), channel_id=1, replica_groups=mesh['parts'=2,'zhi'=8,'zlo'=4,'frame'=4,'head'=2] {'frame','zlo','head'}, dimensions={0} | all-to-all | bytes 262144 | tf_op jit(solution)/shard_map/all_to_all | solution.py:390
  198.5 15.2 %eps_part.5 = bf16[512,128]{1,0:T(8,128)(2,1)} custom-call(bf16[512,128]{1,0:T(8,128)(2,1)} %bitcast.103, f32[448,512]{1,0:T(8,128)} %slice.208.bext_ref, bf16[8,448,64]{2,1,0:T(8,128)(2,1)} %fusion.2.a_ref, f32[8,512]{1,0:T(8,128)} %fusion.32.c_ref, bf16[32,144]{1,0:T(8,128)(2,1)} %pad_maximum_fusion.4.wfp_ref), custom_call_target="tpu_custom_call" | custom-call | flops 1577058304 | tf_op jit(solution)/shard_map/eps_part/pallas_call | solution.py:36
  213.7 13.7 %all_to_all.51.got_ref = bf16[32,16,128]{2,1,0:T(8,128)(2,1)} all-to-all(bf16[32,16,128]{2,1,0:T(8,128)(2,1)} %bitcast.104), channel_id=1, replica_groups=mesh['parts'=2,'zhi'=8,'zlo'=4,'frame'=4,'head'=2] {'frame','zlo','head'}, dimensions={0} | all-to-all | bytes 262144 | tf_op jit(solution)/shard_map/all_to_all | solution.py:372
  227.4 2.3 advance.4
  229.6 13.7 %all_to_all.52 = bf16[32,16,128]{2,1,0:T(8,128)(2,1)} all-to-all(bf16[32,16,128]{2,1,0:T(8,128)(2,1)} %get-tuple-element.15), channel_id=1, replica_groups=mesh['parts'=2,'zhi'=8,'zlo'=4,'frame'=4,'head'=2] {'frame','zlo','head'}, dimensions={0} | all-to-all | bytes 262144 | tf_op jit(solution)/shard_map/all_to_all | solution.py:390
  243.3 15.2 %eps_part.6 = bf16[512,128]{1,0:T(8,128)(2,1)} custom-call(bf16[512,128]{1,0:T(8,128)(2,1)} %bitcast.105, f32[448,512]{1,0:T(8,128)} %slice.208.bext_ref, bf16[8,448,64]{2,1,0:T(8,128)(2,1)} %fusion.2.a_ref, f32[8,512]{1,0:T(8,128)} %fusion.32.c_ref, bf16[32,144]{1,0:T(8,128)(2,1)} %pad_maximum_fusion.4.wfp_ref), custom_call_target="tpu_custom_call" | custom-call | flops 1577058304 | tf_op jit(solution)/shard_map/eps_part/pallas_call | solution.py:36
  258.5 13.7 %all_to_all.53.got_ref = bf16[32,16,128]{2,1,0:T(8,128)(2,1)} all-to-all(bf16[32,16,128]{2,1,0:T(8,128)(2,1)} %bitcast.106), channel_id=1, replica_groups=mesh['parts'=2,'zhi'=8,'zlo'=4,'frame'=4,'head'=2] {'frame','zlo','head'}, dimensions={0} | all-to-all | bytes 262144 | tf_op jit(solution)/shard_map/all_to_all | solution.py:372
  272.2 2.3 advance.5
  274.4 13.7 %all_to_all.54 = bf16[32,16,128]{2,1,0:T(8,128)(2,1)} all-to-all(bf16[32,16,128]{2,1,0:T(8,128)(2,1)} %get-tuple-element.17), channel_id=1, replica_groups=mesh['parts'=2,'zhi'=8,'zlo'=4,'frame'=4,'head'=2] {'frame','zlo','head'}, dimensions={0} | all-to-all | bytes 262144 | tf_op jit(solution)/shard_map/all_to_all | solution.py:390
  288.1 15.2 %eps_part.7 = bf16[512,128]{1,0:T(8,128)(2,1)} custom-call(bf16[512,128]{1,0:T(8,128)(2,1)} %bitcast.102, f32[448,512]{1,0:T(8,128)} %slice.208.bext_ref, bf16[8,448,64]{2,1,0:T(8,128)(2,1)} %fusion.2.a_ref, f32[8,512]{1,0:T(8,128)} %fusion.32.c_ref, bf16[32,144]{1,0:T(8,128)(2,1)} %pad_maximum_fusion.4.wfp_ref), custom_call_target="tpu_custom_call" | custom-call | flops 1577058304 | tf_op jit(solution)/shard_map/eps_part/pallas_call | solution.py:36
  303.3 4.2 %all-to-all-start.8 = ((bf16[32,16,128]{2,1,0:T(8,128)(2,1)}), bf16[32,16,128]{2,1,0:T(8,128)(2,1)S(1)}, u32[]{:S(2)}, u32[]{:S(2)}) async-start(bf16[32,16,128]{2,1,0:T(8,128)(2,1)} %bitcast.101), calls=%async_computation.8 | async-start | bytes 262144 | tf_op jit(solution)/shard_map/all_to_all | solution.py:372
  308.1 8.2 %all-to-all-done.8.got_ref = bf16[32,16,128]{2,1,0:T(8,128)(2,1)S(1)} async-done(((bf16[32,16,128]{2,1,0:T(8,128)(2,1)}), bf16[32,16,128]{2,1,0:T(8,128)(2,1)S(1)}, u32[]{:S(2)}, u32[]{:S(2)}) %all-to-all-start.8) | async-done | bytes 131104 | tf_op jit(solution)/shard_map/all_to_all | solution.py:372
  316.9 2.4 last.1
  319.3 13.7 %all_to_all.55.got_ref = f32[32,8,128]{2,1,0:T(8,128)} all-to-all(f32[32,8,128]{2,1,0:T(8,128)} %last.1), channel_id=1, replica_groups=mesh['parts'=2,'zhi'=8,'zlo'=4,'frame'=4,'head'=2] {'frame','zlo','head'}, dimensions={0} | all-to-all | bytes 262144 | tf_op jit(solution)/shard_map/all_to_all | solution.py:405
  333.0 1.7 end.1
  334.7 1.2 slice_bitcast_fusion.8
  (130 shorter events, 15.5 us)
Async XLA Ops:
  0.6 116.8 %copy-start = (bf16[128,1152]{1,0:T(8,128)(2,1)S(1)}, bf16[128,1152]{1,0:T(8,128)(2,1)}, u32[]{:S(2)}) copy-start(bf16[128,1152]{1,0:T(8,128)(2,1)} %param.14) | copy-start | bytes 884740
  2.4 18.9 %all-to-all-start.1 = ((f32[4,4,144]{2,1,0:T(4,128)}), f32[4,4,144]{2,1,0:T(4,128)S(1)}, u32[]{:S(2)}, u32[]{:S(2)}) async-start(f32[4,4,144]{2,1,0:T(4,128)} %reshape.130), calls=%async_computation.1 | async-start | bytes 32768 | tf_op jit(solution)/shard_map/all_to_all | solution.py:259
  18.9 163.0 %copy-start.5 = (f32[16,128]{1,0:T(8,128)}, f32[16,128]{1,0:T(8,128)S(1)}, u32[]{:S(2)}) copy-start(f32[16,128]{1,0:T(8,128)S(1)} %tile.31.noise_ref) | copy-start | bytes 24580
  22.5 95.3 %all-to-all-start = ((bf16[4,144,1152]{2,1,0:T(8,128)(2,1)}), bf16[4,144,1152]{2,1,0:T(8,128)(2,1)S(1)}, u32[]{:S(2)}, u32[]{:S(2)}) async-start(bf16[4,144,1152]{2,1,0:T(8,128)(2,1)} %broadcast_in_dim.28), calls=%async_computation | async-start | bytes 2654208 | tf_op jit(solution)/shard_map/all_to_all | solution.py:277
  117.4 0.8 copy-start.14
  117.8 7.7 %copy-start.16 = (bf16[8,1152]{1,0:T(8,128)(2,1)}, bf16[8,1152]{1,0:T(8,128)(2,1)S(1)}, u32[]{:S(2)}) copy-start(bf16[8,1152]{1,0:T(8,128)(2,1)S(1)} %get-tuple-element.27) | copy-start | bytes 55300
  118.2 1.1 copy-start.8
  118.2 1.1 copy-start.21
  123.9 1.6 copy-start.7
  127.9 1.6 copy-start.6
  127.9 1.6 copy-start.15
  127.9 1.6 copy-start.17
  127.9 1.6 copy-start.22
  130.8 2.0 copy-start.12
  130.8 2.1 copy-start.13
  139.1 34.3 %copy-start.11 = (bf16[128,128]{1,0:T(8,128)(2,1)S(1)}, bf16[128,128]{1,0:T(8,128)(2,1)}, u32[]{:S(2)}) copy-start(bf16[128,128]{1,0:T(8,128)(2,1)} %mul.142) | copy-start | bytes 98308
  139.1 34.3 %copy-start.10 = (bf16[128,128]{1,0:T(8,128)(2,1)S(1)}, bf16[128,128]{1,0:T(8,128)(2,1)}, u32[]{:S(2)}) copy-start(bf16[128,128]{1,0:T(8,128)(2,1)} %mul.145) | copy-start | bytes 98308
  139.1 34.3 %copy-start.9 = (bf16[128,128]{1,0:T(8,128)(2,1)S(1)}, bf16[128,128]{1,0:T(8,128)(2,1)}, u32[]{:S(2)}) copy-start(bf16[128,128]{1,0:T(8,128)(2,1)} %mul.148) | copy-start | bytes 98308
  139.1 34.4 %copy-start.18 = (f32[32]{0:T(128)S(1)}, f32[32]{0:T(128)}, u32[]{:S(2)}) copy-start(f32[32]{0:T(128)} %get-tuple-element.63) | copy-start | bytes 388
  139.1 34.4 %copy-start.19 = (f32[128]{0:T(128)S(1)}, f32[128]{0:T(128)}, u32[]{:S(2)}) copy-start(f32[128]{0:T(128)} %param.17) | copy-start | bytes 1540
  139.1 34.4 %copy-start.20 = (f32[128]{0:T(128)S(1)}, f32[128]{0:T(128)}, u32[]{:S(2)}) copy-start(f32[128]{0:T(128)} %param.18) | copy-start | bytes 1540
  139.1 35.5 %copy-start.4 = (bf16[16,1152]{1,0:T(8,128)(2,1)S(1)}, bf16[16,1152]{1,0:T(8,128)(2,1)}, u32[]{:S(2)}) copy-start(bf16[16,1152]{1,0:T(8,128)(2,1)} %param.23) | copy-start | bytes 110596
  154.4 27.5 %all-to-all-start.2 = ((bf16[32,16,128]{2,1,0:T(8,128)(2,1)}), bf16[32,16,128]{2,1,0:T(8,128)(2,1)S(1)}, u32[]{:S(2)}, u32[]{:S(2)}) async-start(bf16[32,16,128]{2,1,0:T(8,128)(2,1)} %bitcast.100), calls=%async_computation.2 | async-start | bytes 262144 | tf_op jit(solution)/shard_map/all_to_all | solution.py:372
  173.5 9.1 %copy-start.1 = (bf16[384,128]{1,0:T(8,128)(2,1)}, bf16[384,128]{1,0:T(8,128)(2,1)S(1)}, u32[]{:S(2)}) copy-start(bf16[384,128]{1,0:T(8,128)(2,1)S(1)} %constant_dynamic-update-slice_fusion.3.fblk_ref) | copy-start | bytes 294916
  181.9 0.7 copy-start.3
  303.3 13.0 %all-to-all-start.8 = ((bf16[32,16,128]{2,1,0:T(8,128)(2,1)}), bf16[32,16,128]{2,1,0:T(8,128)(2,1)S(1)}, u32[]{:S(2)}, u32[]{:S(2)}) async-start(bf16[32,16,128]{2,1,0:T(8,128)(2,1)} %bitcast.101), calls=%async_computation.8 | async-start | bytes 262144 | tf_op jit(solution)/shard_map/all_to_all | solution.py:372
  316.3 0.6 copy-start.2

commit v2 on v1

--- a/solution.py
+++ b/solution.py
@@ -12,16 +12,11 @@
 HDIM = 72
 ITERS = 4
 ZLO = 4
+GRANT = 16 * 1024 * 1024
 F32 = jnp.float32
 BF16 = jnp.bfloat16
 STEP = ("zhi", "zlo")
 HOOD = ("frame", "zlo", "head")
-
-
-def three_parts(a):
-    hi = lax.reduce_precision(a, 8, 7)
-    mid = lax.reduce_precision(a - hi, 8, 7)
-    return hi.astype(BF16), mid.astype(BF16), (a - hi - mid).astype(BF16)
 
 
 def chosen(pieces, index):
@@ -40,53 +35,79 @@
         out_specs=jax.tree.map(lambda _: spec, out_shape),
         scratch_shapes=list(scratch),
         cost_estimate=pl.CostEstimate(flops=flops, bytes_accessed=0, transcendentals=0),
+        compiler_params=pltpu.CompilerParams(vmem_limit_bytes=GRANT),
         name=name,
     )(*args)
 
 
-def eps_body(heads, steps, lat, x_ref, bext_ref, a_ref, c_ref, wfp_ref, out_ref, xs, es):
+def eps_body(heads, steps, lat, x_ref, bext_ref, a_ref, c_ref, wfp_ref, out_ref, xs, es, qs, ks, vs, os, s0, s1, m0, m1):
     cols = heads * HDIM
     tokens = x_ref.shape[0]
-    width = bext_ref.shape[0] - lat - 3 * cols
-    assert width == 0
-    model = 1.0 / c_ref.shape[1]
     xs[...] = x_ref[...].astype(F32).T
     scale = math.log2(math.e) / math.sqrt(HDIM)
-    ones16 = jnp.ones((lat, tokens), F32)
+    eight = lax.broadcasted_iota(jnp.int32, (steps, tokens), 0)
+    blank = jnp.zeros((a_ref.shape[1] - 3 * (lat + steps), tokens), F32)
     ones8 = jnp.ones((8, tokens), F32)
-
-    def one_step(step, carry):
+    held, tops = (s0, s1), (m0, m1)
+
+    def project(step, carry):
         rows = pl.ds(pl.multiple_of(step * lat, lat), lat)
         x = xs[rows, :]
-        xcat = jnp.concatenate([x, x, x, ones16], axis=0).astype(BF16)
-        mixed = jnp.dot(a_ref[step], xcat, preferred_element_type=F32) + bext_ref[...]
+        pick = jnp.where(eight == step, 1.0, 0.0)
+        xcat = jnp.concatenate([x, x, x, pick, pick, pick, blank], axis=0).astype(BF16)
+        mixed = jnp.dot(a_ref[...], xcat, preferred_element_type=F32) + bext_ref[...]
         quad = mixed[3 * cols :, :]
         square = jnp.sum(x * quad, axis=0, keepdims=True) + c_ref[pl.ds(step, 1), :]
         rate = lax.rsqrt(jnp.maximum(square, 0.0) + 1e-06)
+        for head in range(heads):
+            q, k, v = (
+                mixed[part * cols + head * HDIM : part * cols + (head + 1) * HDIM, :]
+                for part in range(3)
+            )
+            qs[step, head] = (q * (rate * scale)).astype(BF16)
+            ks[step, head] = (k * rate).astype(BF16)
+            vs[step, head] = jnp.concatenate([v * rate, ones8], axis=0).astype(BF16)
+        return carry
+
+    lax.fori_loop(0, steps, project, 0, unroll=True)
+
+    def score(step, head):
+        s = lax.dot_general(
+            ks[step, head], qs[step, head], (((0,), (0,)), ((), ())), preferred_element_type=F32
+        )
+        held[head % 2][...] = s
+        tops[head % 2][...] = jnp.max(s, axis=0, keepdims=True)
+
+    def weigh(step, head):
+        e = jnp.exp2(held[head % 2][...] - tops[head % 2][...]).astype(BF16)
+        os[step, head] = jnp.dot(vs[step, head], e, preferred_element_type=F32)
+
+    score(0, 0)
+
+    def attend(step, carry):
+        for head in range(heads):
+            if head + 1 < heads:
+                score(step, head + 1)
+            else:
+                score(jnp.minimum(step + 1, steps - 1), 0)
+            weigh(step, head)
+        return carry
+
+    lax.fori_loop(0, steps, attend, 0, unroll=2)
+
+    for step in range(steps):
         outs = []
         for head in range(heads):
-            q = mixed[head * HDIM : (head + 1) * HDIM, :]
-            k = mixed[cols + head * HDIM : cols + (head + 1) * HDIM, :]
-            v = mixed[2 * cols + head * HDIM : 2 * cols + (head + 1) * HDIM, :]
-            q = (q * (rate * scale)).astype(BF16)
-            k = (k * rate).astype(BF16)
-            v = jnp.concatenate([v * rate, ones8], axis=0).astype(BF16)
-            s = lax.dot_general(k, q, (((0,), (0,)), ((), ())), preferred_element_type=F32)
-            top = jnp.max(s, axis=0, keepdims=True)
-            e = jnp.exp2(s - top).astype(BF16)
-            o = jnp.dot(v, e, preferred_element_type=F32)
+            o = os[step, head]
             outs.append(o[:HDIM, :] * (1.0 / o[HDIM : HDIM + 1, :]))
         o = jnp.concatenate(outs, axis=0).astype(BF16)
         part = jnp.dot(wfp_ref[...], o, preferred_element_type=F32)
-        es[rows, :] = part[:lat, :] + part[lat:, :]
-        return carry
-
-    lax.fori_loop(0, steps, one_step, 0)
+        es[step * lat : (step + 1) * lat, :] = part[:lat, :] + part[lat:, :]
     out_ref[...] = es[...].T.astype(BF16)
 
 
 def eps_part(x, bext, a_all, c_all, wfp, lat):
-    steps = a_all.shape[0]
+    steps = c_all.shape[0]
     tokens = x.shape[0]
     heads = wfp.shape[1] // HDIM
     flops = 2 * steps * tokens * (bext.shape[0] * 64 + heads * tokens * 160)
@@ -101,6 +122,14 @@
         scratch=(
             pltpu.VMEM((steps * lat, tokens), F32),
             pltpu.VMEM((steps * lat, tokens), F32),
+            pltpu.VMEM((steps, heads, HDIM, tokens), BF16),
+            pltpu.VMEM((steps, heads, HDIM, tokens), BF16),
+            pltpu.VMEM((steps, heads, HDIM + 8, tokens), BF16),
+            pltpu.VMEM((steps, heads, HDIM + 8, tokens), F32),
+            pltpu.VMEM((tokens, tokens), F32),
+            pltpu.VMEM((tokens, tokens), F32),
+            pltpu.VMEM((1, tokens), F32),
+            pltpu.VMEM((1, tokens), F32),
         ),
         flops=flops,
         name="eps_part",
@@ -212,15 +241,146 @@
     traj_ref[...] = jnp.concatenate(rows, axis=0).T[:lat, :]
 
 
-def smem_first(body, out_shape, where, *args, name=None):
+def smem_first(body, out_shape, where, *args, scratch=(), name=None):
     spec = pl.BlockSpec(memory_space=pltpu.VMEM)
     return pl.pallas_call(
         body,
         out_shape=out_shape,
         in_specs=[pl.BlockSpec(memory_space=pltpu.SMEM)] + [spec] * len(args),
         out_specs=jax.tree.map(lambda _: spec, out_shape),
+        scratch_shapes=list(scratch),
+        compiler_params=pltpu.CompilerParams(vmem_limit_bytes=GRANT),
         name=name,
     )(where, *args)
+
+
+def split_two(a):
+    hi = a.astype(BF16)
+    return hi, (a - hi.astype(F32)).astype(BF16)
+
+
+def split_lanes(a, lat, steps):
+    hi = a.astype(BF16).astype(F32)
+    mid = (a - hi).astype(BF16).astype(F32)
+    low = a - hi - mid
+    lane = lax.broadcasted_iota(jnp.int32, a.shape, 1)
+    first, second, third = 3 * lat, 3 * lat + steps, 3 * lat + 2 * steps
+    is_hi = (lane < lat) | ((lane >= first) & (lane < second))
+    is_mid = ((lane >= lat) & (lane < 2 * lat)) | ((lane >= second) & (lane < third))
+    return jnp.where(is_hi, hi, jnp.where(is_mid, mid, low)).astype(BF16)
+
+
+def prep_body(lat, cores, extra, where_ref, w_ref, all_ref, position_ref, start_ref, index_ref,
+              table_ref, gain_ref, keep_ref, rate_ref, w_in_ref, final_ref,
+              bext_ref, a_ref, c_ref, base_ref, fblk_ref, coef_ref, noise_ref, state_ref, x_ref,
+              temb_ref, turned_ref):
+    zlo, core = where_ref[2], where_ref[3]
+    frames = all_ref.shape[0]
+    rows, model = position_ref.shape
+    groups, mine, lanes = base_ref.shape
+    steps = lanes // lat
+    count = groups * steps
+    inv = 1.0 / model
+    nt = (((1,), (1,)), ((), ()))
+
+    def nt_dot(a, b):
+        return lax.dot_general(a, b, nt, preferred_element_type=F32)
+
+    spots = lax.broadcasted_iota(jnp.int32, (count, table_ref.shape[0]), 1).astype(F32)
+    pick_time = jnp.where(index_ref[:, 0:1] == spots, 1.0, 0.0).astype(BF16)
+    pick_sched = jnp.where(index_ref[:, 1:2] == spots, 1.0, 0.0)
+    temb_all = jnp.dot(pick_time, table_ref[...], preferred_element_type=F32)
+    temb_ref[...] = temb_all
+    temb = temb_ref[pl.ds(pl.multiple_of(zlo * steps, steps), steps), :]
+    lane = lax.broadcasted_iota(jnp.int32, (count, lanes), 1)
+    own = lax.broadcasted_iota(jnp.int32, (count, lanes), 0)
+    here = (lane // lat) == lax.rem(own, steps)
+
+    def spread(a):
+        return jnp.sum(jnp.where(here, a, 0.0).reshape(groups, steps, lanes), axis=1)
+
+    keep = jnp.sum(pick_sched * keep_ref[...], axis=1, keepdims=True)
+    rate = jnp.sum(pick_sched * rate_ref[...], axis=1, keepdims=True)
+    coef_ref[:groups] = spread(jnp.broadcast_to(keep, (count, lanes)))
+    coef_ref[groups:] = spread(jnp.broadcast_to(rate, (count, lanes)))
+
+    final = final_ref[...].astype(F32)
+    final = jnp.concatenate([final] * steps, axis=0).astype(BF16)
+    w_in = w_in_ref[...].astype(F32)
+    w_in_all = jnp.concatenate([w_in] * steps, axis=0).astype(BF16)
+    mixed = nt_dot(w_in_all, final)
+    square_lane = lax.broadcasted_iota(jnp.int32, (lanes, lanes), 1) // lat
+    square_row = lax.broadcasted_iota(jnp.int32, (lanes, lanes), 0) // lat
+    mixed = jnp.where(square_lane == square_row, mixed, 0.0)
+    hi = mixed.astype(BF16)
+    mid = (mixed - hi.astype(F32)).astype(BF16)
+    fblk_ref[:lanes] = hi
+    fblk_ref[lanes : 2 * lanes] = mid
+    fblk_ref[2 * lanes :] = (mixed - hi.astype(F32) - mid.astype(F32)).astype(BF16)
+    at = pl.multiple_of((zlo * cores + core) * mine, mine)
+    base_own = nt_dot(position_ref[pl.ds(at, mine), :], final)
+    base_time = spread(nt_dot(temb_all.astype(BF16), final))
+    for group in range(groups):
+        base_ref[group] = base_own + base_time[group : group + 1, :]
+
+    turned_ref[...] = jnp.concatenate([start_ref[...]] * steps, axis=0).T
+    noise = turned_ref[pl.ds(at, mine), :]
+    noise_ref[...] = noise
+    for group in range(groups):
+        state_ref[group] = noise
+    for frame in range(frames):
+        noise = all_ref[frame, rows:, :rows].astype(F32)
+        x_ref[frame * rows : (frame + 1) * rows] = (
+            jnp.concatenate([noise] * steps, axis=0).T.astype(BF16)
+        )
+
+    blank = jnp.zeros((lanes - 3 * (lat + steps), model), F32)
+    thin = jnp.concatenate([w_in, w_in, w_in, temb, temb, temb, blank], axis=0)
+    thin_bf = thin.astype(BF16)
+    gain = gain_ref[...]
+    w = w_ref[...]
+    thin_hi, thin_lo = split_two(thin * gain)
+    linear = jnp.dot(thin_hi, w, preferred_element_type=F32) + jnp.dot(
+        thin_lo, w, preferred_element_type=F32
+    )
+    places = []
+    for part in range(3):
+        places += [(part * lanes, lanes), (3 * lanes + part * extra, extra)]
+    row = 0
+    turned = linear.T
+    for start, size in places:
+        a_ref[row : row + size] = split_lanes(turned[start : start + size], lat, steps)
+        row += size
+    gram = nt_dot(thin_bf[:lat], thin_bf)
+    gram_lane = lax.broadcasted_iota(jnp.int32, gram.shape, 1)
+    gram = gram * jnp.where(gram_lane < 3 * lat, inv, 2.0 * inv)
+    a_ref[row:] = split_lanes(gram, lat, steps)
+    temb_square = jnp.sum(temb * temb, axis=1, keepdims=True)
+    for frame in range(frames):
+        there = pl.ds(frame * rows, rows)
+        tokens_bf = all_ref[frame, :rows, :]
+        wide = tokens_bf.astype(F32)
+        wide_hi, wide_lo = split_two(wide * gain)
+        linear = (
+            jnp.dot(wide_hi, w, preferred_element_type=F32)
+            + jnp.dot(wide_lo, w, preferred_element_type=F32)
+        ).T
+        row = 0
+        for start, size in places:
+            bext_ref[row : row + size, frame * rows : (frame + 1) * rows] = linear[
+                start : start + size
+            ]
+            row += size
+        gram = nt_dot(thin_bf, tokens_bf)
+        bext_ref[row:, frame * rows : (frame + 1) * rows] = gram[:lat] * (2.0 * inv)
+        square = wide * wide
+        folded = square[:, :lanes]
+        for chunk in range(1, model // lanes):
+            folded = folded + square[:, chunk * lanes : (chunk + 1) * lanes]
+        square = jnp.sum(folded.T, axis=0, keepdims=True)
+        c_ref[:, frame * rows : (frame + 1) * rows] = inv * (
+            square + 2.0 * gram[3 * lat : 3 * lat + steps] + temb_square
+        )
 
 
 def local(
@@ -277,96 +437,51 @@
     frame_all = lax.all_to_all(
         jnp.broadcast_to(frame_load[None], (frames, *frame_load.shape)), "frame", 0, 0, tiled=True
     )
-    positions = frame_all[:, :row_count].reshape(tokens, model)
-    noise_all = frame_all[:, row_count:, :row_count]
-
-    w_main = [
-        gathered[:, k * rows_d : (k + 1) * rows_d].reshape(step_n * rows_d, lanes) for k in range(3)
-    ]
     sides = gathered[:, 3 * rows_d : 3 * rows_d + tall]
     extra = cols - lanes
     w_rest = jnp.concatenate([sides[:, :, : 3 * extra], sides[:, :, 3 * extra : 6 * extra]], axis=1)
-    w_rest = w_rest.reshape(step_n * rows_d, 3 * extra)
+    w_rest = jnp.pad(w_rest, ((0, 0), (0, 0), (0, lanes - 3 * extra)))
+    w_all = jnp.concatenate(
+        [gathered[:, k * rows_d : (k + 1) * rows_d] for k in range(3)] + [w_rest], axis=2
+    ).reshape(step_n * rows_d, 4 * lanes)
     part = lat // zlo_n
     mixes = sides[:, :, 6 * extra :].astype(F32).reshape(zhi_n, zlo_n, tall, pieces, part)
     mixes = jnp.sum(mixes, axis=0).transpose(0, 3, 2, 1).reshape(lat, cols)
     mix_hi = lax.reduce_precision(mixes, 8, 7)
     wfp = jnp.concatenate([mix_hi, mixes - mix_hi], axis=0).astype(BF16)
-    table_rows = time_table.shape[0]
-    indices = gathered[:, 3 * rows_d + tall, :2].astype(F32)
-    spots = jnp.arange(table_rows, dtype=F32)
-    pick_time = (indices[:, :1] == spots[None]).astype(BF16)
-    pick_sched = (indices[:, 1:] == spots[None]).astype(F32)
-    temb_all = jnp.dot(pick_time, time_table, preferred_element_type=F32).astype(BF16)
-    keep = jnp.sum(pick_sched * coef_keep[None], axis=1)
-    rate = jnp.sum(pick_sched * coef_noise[None], axis=1)
-    coef = jnp.repeat(jnp.concatenate([keep, rate]).reshape(2 * zlo_n, steps), lat, axis=1)
-    temb = lax.dynamic_slice_in_dim(temb_all, zlo * steps, steps, 0)
-
-    every = jnp.concatenate([positions, w_in, temb], axis=0)
-    scaled = every.astype(F32) * norm_gain[None]
-    scaled_hi = lax.reduce_precision(scaled, 8, 7)
-    scaled_lo = (scaled - scaled_hi).astype(BF16)
-    scaled_hi = scaled_hi.astype(BF16)
-
-    def against(w):
-        dims = (((0,), (1,)), ((), ()))
-        return lax.dot_general(w, scaled_hi, dims, preferred_element_type=F32) + lax.dot_general(
-            w, scaled_lo, dims, preferred_element_type=F32
-        )
-
-    thin = against(w_rest)
-    blocks = []
-    for k in range(3):
-        blocks += [against(w_main[k]), thin[k * extra : (k + 1) * extra]]
-    gram = lax.dot_general(
-        jnp.concatenate([w_in, temb], axis=0),
-        every,
-        (((1,), (1,)), ((), ())),
-        preferred_element_type=F32,
-    )
-    inv = 1.0 / model
-    linear = jnp.concatenate(
-        blocks + [gram[:lat] * jnp.where(jnp.arange(every.shape[0]) // lat == tokens // lat, inv, 2 * inv)],
-        axis=0,
-    )
-    bext = linear[:, :tokens]
-    latent = linear[:, tokens : tokens + lat]
-    time_part = linear[:, tokens + lat :]
-    latent_parts = jnp.concatenate(three_parts(latent), axis=1)
-    time_parts = jnp.stack(three_parts(time_part.T), axis=2)
-    a_all = jnp.concatenate(
-        [
-            jnp.broadcast_to(latent_parts[None], (steps, *latent_parts.shape)),
-            jnp.pad(time_parts, ((0, 0), (0, 0), (0, lat - 3))),
-        ],
-        axis=2,
-    )
-    wide = positions.astype(F32)
-    temb_wide = temb.astype(F32)
-    c_all = (
-        jnp.sum(wide * wide, axis=1)[None]
-        + 2.0 * gram[lat:, :tokens]
-        + jnp.sum(temb_wide * temb_wide, axis=1)[:, None]
-    ) * inv
-
-    at = (zlo * cores + core) * mine
-    own_position = lax.dynamic_slice_in_dim(position, at, mine, 0)
-    own_noise = lax.dynamic_slice_in_dim(start_noise, at, mine, 1).T
-    nt = (((1,), (1,)), ((), ()))
-    base_own = lax.dot_general(own_position, w_final, nt, preferred_element_type=F32)
-    base_time = lax.dot_general(temb_all, w_final, nt, preferred_element_type=F32)
-    base = jnp.tile(base_own, (1, steps))[None] + base_time.reshape(zlo_n, 1, lanes)
-    final_in = lax.dot_general(w_in, w_final, nt, preferred_element_type=F32)
-    fblk = jnp.concatenate(
-        [jnp.kron(jnp.eye(steps, dtype=F32), p.astype(F32)) for p in three_parts(final_in)], axis=0
-    ).astype(BF16)
-    noise = jnp.tile(own_noise, (1, steps))
-    states = jnp.broadcast_to(noise[None], (zlo_n, mine, lanes))
-    x = jnp.tile(noise_all.transpose(0, 2, 1).reshape(tokens, lat), (1, steps))
+    index_rows = gathered[:, 3 * rows_d + tall].astype(F32)
+
+    where = jnp.stack([zhi, frame, zlo, core]).astype(jnp.int32)
+    bext, a_all, c_all, base, fblk, coef, noise, states, x = smem_first(
+        functools.partial(prep_body, lat, cores, extra),
+        (
+            jax.ShapeDtypeStruct((3 * cols + lat, tokens), F32),
+            jax.ShapeDtypeStruct((3 * cols + lat, lanes), BF16),
+            jax.ShapeDtypeStruct((steps, tokens), F32),
+            jax.ShapeDtypeStruct((zlo_n, mine, lanes), F32),
+            jax.ShapeDtypeStruct((3 * lanes, lanes), BF16),
+            jax.ShapeDtypeStruct((2 * zlo_n, lanes), F32),
+            jax.ShapeDtypeStruct((mine, lanes), F32),
+            jax.ShapeDtypeStruct((zlo_n, mine, lanes), F32),
+            jax.ShapeDtypeStruct((tokens, lanes), BF16),
+        ),
+        where,
+        w_all,
+        frame_all,
+        position,
+        start_noise,
+        index_rows,
+        time_table,
+        norm_gain[None],
+        coef_keep[None],
+        coef_noise[None],
+        w_in,
+        w_final,
+        scratch=(pltpu.VMEM((step_n, model), F32), pltpu.VMEM((row_count, lanes), F32)),
+        name="prep",
+    )
 
     squares = []
-    where = jnp.stack([zhi, frame, zlo]).astype(jnp.int32)
     for iteration in range(ITERS):
         part_eps = eps_part(x, bext, a_all, c_all, wfp, lat)
         got = lax.all_to_all(part_eps.reshape(members, mine, lanes), HOOD, 0, 0, tiled=True)

time: 338 us -> 265 us (0.78)
  Pallas kernels: 71.6 us -> 39.4 us
  blocking collectives: 166 us -> 197 us
  starting transfers between devices: 36.5 us -> 13.3 us
  local copies, waits for them, and re-layouts: 21.4 us -> 6.69 us
  waiting for transfers between devices: 14.6 us -> 0.01 us
  matrix products: 13.4 us -> 1.09 us
  other arithmetic: 9.34 us -> 4.83 us
    all_to_all x2 -> x4, blocking collectives: 27.3 us -> 63.8 us  [local(): lax.all_to_all(part_eps.reshape(members, mine, lanes), HOOD, 0, 0, tiled=...]
    pallas_call x7, Pallas kernels: 67.5 us -> 33.5 us  [vmem_call(): pl.pallas_call(body, out_shape=out_shape, in_specs=[spec] * len(args), ou...]
    all_to_all x2 -> x0, starting transfers between devices: 23.2 us -> none  [local(): lax.all_to_all(part_eps.reshape(members, mine, lanes), HOOD, 0, 0, tiled=...]
    all_to_all x2 -> x0, waiting for transfers between devices: 14.6 us -> none  [local(): lax.all_to_all(part_eps.reshape(members, mine, lanes), HOOD, 0, 0, tiled=...]
    dot_general x13 -> x0, matrix products: 12.3 us -> none  [the longest x4 4.96 us: against(): lax.dot_general(w, scaled_lo, dims, preferred_element_type=F32)]
    all_to_all x3, blocking collectives: 41 us -> 36.5 us  [local(): x = lax.all_to_all(send, HOOD, 0, 0, tiled=True).reshape(tokens, lanes)]
    add x4 -> x0, local copies, waits for them, and re-layouts: 3.47 us -> none  [the longest x3 3.38 us: against(): lax.dot_general(w, scaled_hi, dims, preferred_element_type=F32)]
  transfers between devices with their start and end apart: 4 -> 2, of which waited for: 2 -> 0; matrix products, arithmetic and copies ran while one was open for 5% -> 3% of each run, Pallas kernels for 0% -> 0%
where the time goes in v2:
time: 265 us
  blocking collectives  197 us (74%)
  Pallas kernels  39.4 us (15%)
  starting transfers between devices  13.3 us (5%)
  local copies, waits for them, and re-layouts  6.69 us (3%)
  other arithmetic  4.83 us (2%)
    all_gather x1, blocking collectives, local(): gathered = lax.all_gather(payload, STEP, axis=0)  84.4 us
    all_to_all x4, blocking collectives, local(): lax.all_to_all(part_eps.reshape(members, mine, lanes), HOOD, 0, 0, tiled=...  63.8 us
    all_to_all x3, blocking collectives, local(): x = lax.all_to_all(send, HOOD, 0, 0, tiled=True).reshape(tokens, lanes)  36.5 us
    pallas_call x7, Pallas kernels, vmem_call(): pl.pallas_call(body, out_shape=out_shape, in_specs=[spec] * len(args), ou...  33.5 us
    all_to_all x1, blocking collectives, local(): ended = lax.all_to_all(send, HOOD, 0, 0, tiled=True)  12.2 us
    all_to_all x1, starting transfers between devices, local(): lax.all_to_all(mix.reshape(zlo_n, lat // zlo_n, cols), 'zlo', 0, 0, tiled...  9.02 us
    pallas_call x3, Pallas kernels, smem_first(): pl.pallas_call(body, out_shape=out_shape, in_specs=[pl.BlockSpec(memory_s...  5.95 us
  transfers between devices with their start and end apart: 2, of which 0 were waited for; matrix products, arithmetic and copies ran while one was open for 3% of the time, Pallas kernels for 0%

profile of v2, /device:TPU:33, one launch (start us, length us, event | category | flops | bytes accessed | tf_op | source)
XLA Modules:
  0.0 264.5 jit_solution(2197232811812536632)
XLA Ops:
  0.7 1.1 fusion.5
  1.7 0.6 reshape.43
  2.4 9.0 %all-to-all-start = ((f32[4,4,144]{2,1,0:T(4,128)}), f32[4,4,144]{2,1,0:T(4,128)S(1)}, u32[]{:S(2)}, u32[]{:S(2)}) async-start(f32[4,4,144]{2,1,0:T(4,128)} %reshape.43), calls=%async_computation | async-start | bytes 32768 | tf_op jit(solution)/shard_map/all_to_all | solution.py:419
  11.4 1.2 select_select_fusion
  13.9 0.7 convert_element_type.25
  14.6 0.1 pad_maximum_fusion.2
  14.8 1.0 fusion.3
  15.7 0.1 pad_add_fusion.where_ref
  15.8 1.2 broadcast_in_dim.22
  17.0 4.3 %all-to-all-start.1 = ((bf16[4,144,1152]{2,1,0:T(8,128)(2,1)}), bf16[4,144,1152]{2,1,0:T(8,128)(2,1)S(1)}, u32[]{:S(2)}, u32[]{:S(2)}) async-start(bf16[4,144,1152]{2,1,0:T(8,128)(2,1)} %broadcast_in_dim.22), calls=%async_computation.1 | async-start | bytes 2654208 | tf_op jit(solution)/shard_map/all_to_all | solution.py:437
  21.4 0.1 copy.24
  21.5 0.1 copy.23
  21.6 0.1 copy.22
  21.8 0.1 copy.21
  21.9 0.1 copy.20
  22.0 0.1 copy.19
  22.1 0.1 copy.18
  22.2 0.1 copy.17
  22.3 0.1 concatenate.27
  22.4 0.3 concatenate.29
  22.8 84.4 %all-gather.1 = bf16[32,127,128]{2,1,0:T(8,128)(2,1)S(1)} all-gather(bf16[1,127,128]{2,1,0:T(8,128)(2,1)S(1)} %bitcast.55), channel_id=2, replica_groups=mesh['parts'=2,'zhi'=8,'zlo'=4,'frame'=4,'head'=2] {'zhi','zlo'}, dimensions={0}, use_global_device_ids=true | all-gather | bytes 1072896 | tf_op jit(solution)/shard_map/all_gather | solution.py:433
  107.2 0.1 slice.154
  107.4 0.1 fusion.23
  107.5 0.3 copy.29
  107.8 0.2 convert_reduce_fusion
  108.0 0.1 reshape.47
  108.1 0.3 fusion.22
  108.4 1.2 pad_maximum_fusion
  109.7 2.2 reshape.44.w_ref
  112.0 3.4 %prep.1 = (f32[448,512]{1,0:T(8,128)S(1)}, bf16[448,128]{1,0:T(8,128)(2,1)S(1)}, f32[8,512]{1,0:T(8,128)S(1)}, f32[4,16,128]{2,1,0:T(8,128)S(1)}, bf16[384,128]{...) custom-call(s32[4]{0:T(128)S(1)} %pad_add_fusion.where_ref, ...), custom_call_target="tpu_custom_call" | custom-call | tf_op jit(solution)/shard_map/prep/pallas_call | solution.py:246
  115.5 7.9 %eps_part.4 = bf16[512,128]{1,0:T(8,128)(2,1)S(1)} custom-call(bf16[512,128]{1,0:T(8,128)(2,1)S(1)} %get-tuple-element.22.x_ref, f32[448,512]{1,0:T(8,128)S(1)} %get-tuple-element.23.bext_ref, bf16[448,128]{1,0:T(8,128)(2,1)S(1)} %get-tuple-element.24.a_ref, f32[8,512]{1,0:T(8,128)S(1)} %get-tuple-element.25.c_ref, bf16[32,144]{1,0:T(8,128)(2,1)S(1)} %pad_maximum_fusion.1.wfp_ref), custom_call_target="tpu_custom_call" | custom-call | flops 1577058304 | tf_op jit(solution)/shard_map/eps_part/pallas_call | solution.py:31
  123.4 27.3 %all_to_all.50.got_ref = bf16[32,16,128]{2,1,0:T(8,128)(2,1)S(1)} all-to-all(bf16[32,16,128]{2,1,0:T(8,128)(2,1)S(1)} %bitcast.46), channel_id=1, replica_groups=mesh['parts'=2,'zhi'=8,'zlo'=4,'frame'=4,'head'=2] {'frame','zlo','head'}, dimensions={0} | all-to-all | bytes 262144 | tf_op jit(solution)/shard_map/all_to_all | solution.py:487
  150.7 0.6 advance.3
  151.3 12.2 %all_to_all.51 = bf16[32,16,128]{2,1,0:T(8,128)(2,1)S(1)} all-to-all(bf16[32,16,128]{2,1,0:T(8,128)(2,1)S(1)} %get-tuple-element.31), channel_id=1, replica_groups=mesh['parts'=2,'zhi'=8,'zlo'=4,'frame'=4,'head'=2] {'frame','zlo','head'}, dimensions={0} | all-to-all | bytes 262144 | tf_op jit(solution)/shard_map/all_to_all | solution.py:505
  163.5 7.9 %eps_part.5 = bf16[512,128]{1,0:T(8,128)(2,1)S(1)} custom-call(bf16[512,128]{1,0:T(8,128)(2,1)S(1)} %bitcast.47, f32[448,512]{1,0:T(8,128)S(1)} %get-tuple-element.23.bext_ref, bf16[448,128]{1,0:T(8,128)(2,1)S(1)} %get-tuple-element.24.a_ref, f32[8,512]{1,0:T(8,128)S(1)} %get-tuple-element.25.c_ref, bf16[32,144]{1,0:T(8,128)(2,1)S(1)} %pad_maximum_fusion.1.wfp_ref), custom_call_target="tpu_custom_call" | custom-call | flops 1577058304 | tf_op jit(solution)/shard_map/eps_part/pallas_call | solution.py:31
  171.4 12.2 %all_to_all.52.got_ref = bf16[32,16,128]{2,1,0:T(8,128)(2,1)S(1)} all-to-all(bf16[32,16,128]{2,1,0:T(8,128)(2,1)S(1)} %bitcast.48), channel_id=1, replica_groups=mesh['parts'=2,'zhi'=8,'zlo'=4,'frame'=4,'head'=2] {'frame','zlo','head'}, dimensions={0} | all-to-all | bytes 262144 | tf_op jit(solution)/shard_map/all_to_all | solution.py:487
  183.6 0.6 advance.4
  184.2 12.2 %all_to_all.53 = bf16[32,16,128]{2,1,0:T(8,128)(2,1)S(1)} all-to-all(bf16[32,16,128]{2,1,0:T(8,128)(2,1)S(1)} %get-tuple-element.33), channel_id=1, replica_groups=mesh['parts'=2,'zhi'=8,'zlo'=4,'frame'=4,'head'=2] {'frame','zlo','head'}, dimensions={0} | all-to-all | bytes 262144 | tf_op jit(solution)/shard_map/all_to_all | solution.py:505
  196.3 7.9 %eps_part.6 = bf16[512,128]{1,0:T(8,128)(2,1)S(1)} custom-call(bf16[512,128]{1,0:T(8,128)(2,1)S(1)} %bitcast.49, f32[448,512]{1,0:T(8,128)S(1)} %get-tuple-element.23.bext_ref, bf16[448,128]{1,0:T(8,128)(2,1)S(1)} %get-tuple-element.24.a_ref, f32[8,512]{1,0:T(8,128)S(1)} %get-tuple-element.25.c_ref, bf16[32,144]{1,0:T(8,128)(2,1)S(1)} %pad_maximum_fusion.1.wfp_ref), custom_call_target="tpu_custom_call" | custom-call | flops 1577058304 | tf_op jit(solution)/shard_map/eps_part/pallas_call | solution.py:31
  204.3 12.2 %all_to_all.54.got_ref = bf16[32,16,128]{2,1,0:T(8,128)(2,1)S(1)} all-to-all(bf16[32,16,128]{2,1,0:T(8,128)(2,1)S(1)} %bitcast.50), channel_id=1, replica_groups=mesh['parts'=2,'zhi'=8,'zlo'=4,'frame'=4,'head'=2] {'frame','zlo','head'}, dimensions={0} | all-to-all | bytes 262144 | tf_op jit(solution)/shard_map/all_to_all | solution.py:487
  216.4 0.6 advance.5
  217.0 12.2 %all_to_all.55 = bf16[32,16,128]{2,1,0:T(8,128)(2,1)S(1)} all-to-all(bf16[32,16,128]{2,1,0:T(8,128)(2,1)S(1)} %get-tuple-element.35), channel_id=1, replica_groups=mesh['parts'=2,'zhi'=8,'zlo'=4,'frame'=4,'head'=2] {'frame','zlo','head'}, dimensions={0} | all-to-all | bytes 262144 | tf_op jit(solution)/shard_map/all_to_all | solution.py:505
  229.2 7.9 %eps_part.7 = bf16[512,128]{1,0:T(8,128)(2,1)S(1)} custom-call(bf16[512,128]{1,0:T(8,128)(2,1)S(1)} %bitcast.44, f32[448,512]{1,0:T(8,128)S(1)} %get-tuple-element.23.bext_ref, bf16[448,128]{1,0:T(8,128)(2,1)S(1)} %get-tuple-element.24.a_ref, f32[8,512]{1,0:T(8,128)S(1)} %get-tuple-element.25.c_ref, bf16[32,144]{1,0:T(8,128)(2,1)S(1)} %pad_maximum_fusion.1.wfp_ref), custom_call_target="tpu_custom_call" | custom-call | flops 1577058304 | tf_op jit(solution)/shard_map/eps_part/pallas_call | solution.py:31
  237.1 12.2 %all_to_all.56.got_ref = bf16[32,16,128]{2,1,0:T(8,128)(2,1)S(1)} all-to-all(bf16[32,16,128]{2,1,0:T(8,128)(2,1)S(1)} %bitcast.45), channel_id=1, replica_groups=mesh['parts'=2,'zhi'=8,'zlo'=4,'frame'=4,'head'=2] {'frame','zlo','head'}, dimensions={0} | all-to-all | bytes 262144 | tf_op jit(solution)/shard_map/all_to_all | solution.py:487
  249.3 1.3 last.1
  250.6 12.2 %all_to_all.57.got_ref = f32[32,8,128]{2,1,0:T(8,128)S(1)} all-to-all(f32[32,8,128]{2,1,0:T(8,128)S(1)} %last.1), channel_id=1, replica_groups=mesh['parts'=2,'zhi'=8,'zlo'=4,'frame'=4,'head'=2] {'frame','zlo','head'}, dimensions={0} | all-to-all | bytes 262144 | tf_op jit(solution)/shard_map/all_to_all | solution.py:520
  262.7 1.3 end.1
  264.0 0.5 slice_bitcast_fusion.6
  (30 shorter events, 0.3 us)
Async XLA Ops:
  0.6 15.2 %copy-start.7 = (f32[1152]{0:T(1024)S(1)}, f32[1152]{0:T(1024)}, u32[]{:S(2)}) copy-start(f32[1152]{0:T(1024)} %param.20) | copy-start | bytes 13828
  2.4 13.5 %all-to-all-start = ((f32[4,4,144]{2,1,0:T(4,128)}), f32[4,4,144]{2,1,0:T(4,128)S(1)}, u32[]{:S(2)}, u32[]{:S(2)}) async-start(f32[4,4,144]{2,1,0:T(4,128)} %reshape.43), calls=%async_computation | async-start | bytes 32768 | tf_op jit(solution)/shard_map/all_to_all | solution.py:419
  17.0 94.9 %all-to-all-start.1 = ((bf16[4,144,1152]{2,1,0:T(8,128)(2,1)}), bf16[4,144,1152]{2,1,0:T(8,128)(2,1)S(1)}, u32[]{:S(2)}, u32[]{:S(2)}) async-start(bf16[4,144,1152]{2,1,0:T(8,128)(2,1)} %broadcast_in_dim.22), calls=%async_computation.1 | async-start | bytes 2654208 | tf_op jit(solution)/shard_map/all_to_all | solution.py:437
  109.7 2.3 copy-start
  109.7 2.3 copy-start.1
  109.7 2.3 copy-start.2
  109.7 2.3 copy-start.3
  109.7 2.3 copy-start.4
  109.7 2.3 copy-start.5
  109.7 2.3 copy-start.6

commit v3 on v2

--- a/solution.py
+++ b/solution.py
@@ -49,6 +49,8 @@
     blank = jnp.zeros((a_ref.shape[1] - 3 * (lat + steps), tokens), F32)
     ones8 = jnp.ones((8, tokens), F32)
     held, tops = (s0, s1), (m0, m1)
+
+    lanes_pad = 128
 
     def project(step, carry):
         rows = pl.ds(pl.multiple_of(step * lat, lat), lat)
@@ -65,16 +67,14 @@
                 for part in range(3)
             )
             qs[step, head] = (q * (rate * scale)).astype(BF16)
-            ks[step, head] = (k * rate).astype(BF16)
+            ks[step, head] = (jnp.concatenate([k * rate, jnp.zeros((lanes_pad - HDIM, tokens), F32)], axis=0).T).astype(BF16)
             vs[step, head] = jnp.concatenate([v * rate, ones8], axis=0).astype(BF16)
         return carry
 
     lax.fori_loop(0, steps, project, 0, unroll=True)
 
     def score(step, head):
-        s = lax.dot_general(
-            ks[step, head], qs[step, head], (((0,), (0,)), ((), ())), preferred_element_type=F32
-        )
+        s = jnp.dot(ks[step, head][:, :HDIM], qs[step, head], preferred_element_type=F32)
         held[head % 2][...] = s
         tops[head % 2][...] = jnp.max(s, axis=0, keepdims=True)
 
@@ -123,7 +123,7 @@
             pltpu.VMEM((steps * lat, tokens), F32),
             pltpu.VMEM((steps * lat, tokens), F32),
             pltpu.VMEM((steps, heads, HDIM, tokens), BF16),
-            pltpu.VMEM((steps, heads, HDIM, tokens), BF16),
+            pltpu.VMEM((steps, heads, tokens, 128), BF16),
             pltpu.VMEM((steps, heads, HDIM + 8, tokens), BF16),
             pltpu.VMEM((steps, heads, HDIM + 8, tokens), F32),
             pltpu.VMEM((tokens, tokens), F32),
@@ -270,10 +270,9 @@
     return jnp.where(is_hi, hi, jnp.where(is_mid, mid, low)).astype(BF16)
 
 
-def prep_body(lat, cores, extra, where_ref, w_ref, all_ref, position_ref, start_ref, index_ref,
-              table_ref, gain_ref, keep_ref, rate_ref, w_in_ref, final_ref,
-              bext_ref, a_ref, c_ref, base_ref, fblk_ref, coef_ref, noise_ref, state_ref, x_ref,
-              temb_ref, turned_ref):
+def prep_body(lat, cores, extra, where_ref, got_ref, all_ref, position_ref, start_ref, table_ref,
+              gain_ref, keep_ref, rate_ref, w_in_ref, final_ref, bext_ref, a_ref, c_ref, base_ref, fblk_ref, coef_ref, noise_ref, state_ref, x_ref,
+              temb_ref, turned_ref, w_ref, index_ref):
     zlo, core = where_ref[2], where_ref[3]
     frames = all_ref.shape[0]
     rows, model = position_ref.shape
@@ -285,6 +284,22 @@
 
     def nt_dot(a, b):
         return lax.dot_general(a, b, nt, preferred_element_type=F32)
+
+    rows_d = model // count
+    tall = rows_d // 2
+    for source in range(count):
+        got = got_ref[source].astype(F32)
+        at = source * rows_d
+        for part in range(3):
+            w_ref[at : at + rows_d, part * lanes : (part + 1) * lanes] = got[
+                part * rows_d : (part + 1) * rows_d
+            ]
+        side = got[3 * rows_d : 3 * rows_d + tall]
+        w_ref[at : at + tall, 3 * lanes :] = side
+        w_ref[at + tall : at + rows_d, 3 * lanes :] = jnp.concatenate(
+            [side[:, 3 * extra :], side[:, : 3 * extra]], axis=1
+        )
+        index_ref[source : source + 1] = got[3 * rows_d + tall : 3 * rows_d + tall + 1]
 
     spots = lax.broadcasted_iota(jnp.int32, (count, table_ref.shape[0]), 1).astype(F32)
     pick_time = jnp.where(index_ref[:, 0:1] == spots, 1.0, 0.0).astype(BF16)
@@ -338,7 +353,7 @@
     thin = jnp.concatenate([w_in, w_in, w_in, temb, temb, temb, blank], axis=0)
     thin_bf = thin.astype(BF16)
     gain = gain_ref[...]
-    w = w_ref[...]
+    w = w_ref[...].astype(BF16)
     thin_hi, thin_lo = split_two(thin * gain)
     linear = jnp.dot(thin_hi, w, preferred_element_type=F32) + jnp.dot(
         thin_lo, w, preferred_element_type=F32
@@ -383,6 +398,63 @@
         )
 
 
+def exact_pick(values, wanted):
+    return jnp.dot(values, jnp.where(wanted, 1.0, 0.0).astype(BF16), preferred_element_type=F32)
+
+
+def pack_body(extra, where_ref, qkv_ref, proj_ref, final_ref, start_ref, position_ref,
+              mix_ref, frame_ref, main_ref, rows_ref, half_ref):
+    frame, step = where_ref[1], where_ref[4]
+    lat, rows = start_ref.shape
+    rows_d, width = proj_ref.shape
+    frames, parts = frame_ref.shape[0], mix_ref.shape[0]
+    lanes = main_ref.shape[1]
+    cols = mix_ref.shape[2]
+    tall = rows_d // 2
+
+    column = lax.broadcasted_iota(jnp.int32, (width, 2 * lanes), 0) - frame * cols
+    lane = lax.broadcasted_iota(jnp.int32, (width, 2 * lanes), 1)
+    both = column == lane
+    model = final_ref.shape[1]
+    feature = lax.broadcasted_iota(jnp.int32, (model, lanes), 0) - step * rows_d
+    final = exact_pick(final_ref[...], feature == lax.broadcasted_iota(jnp.int32, (model, lanes), 1))
+    proj = exact_pick(proj_ref[...], both)
+    blank = jnp.zeros((lanes - rows_d, 2 * lanes), F32)
+    proj = jnp.concatenate([proj, blank], axis=0).astype(BF16)
+    feature_lane = lax.broadcasted_iota(jnp.int32, final.shape, 1)
+    final = jnp.where(feature_lane < rows_d, final, 0.0).astype(BF16)
+    mix = jnp.dot(final, proj, preferred_element_type=F32)
+    each = lat // parts
+    for part in range(parts):
+        mix_ref[part] = mix[part * each : (part + 1) * each, :cols]
+
+    noise = jnp.concatenate(
+        [start_ref[...], jnp.zeros((lat, model - rows), F32)], axis=1
+    ).astype(BF16)
+    for at in range(frames):
+        frame_ref[at, :rows] = position_ref[...]
+        frame_ref[at, rows:] = noise
+
+    side = jnp.zeros((rows_d, 2 * lanes), F32)
+    for part in range(3):
+        weights = qkv_ref[part]
+        rows_ref[part * rows_d : (part + 1) * rows_d, :] = exact_pick(weights, both)[:, :lanes]
+        shifted = lane - part * extra
+        first = (column - lanes == shifted) & (shifted >= 0) & (shifted < extra)
+        shifted = lane - lanes - (3 + part) * extra
+        second = (column - lanes == shifted) & (shifted >= 0) & (shifted < extra)
+        side = side + exact_pick(weights, first | second)
+    half_ref[...] = side[:, lanes:]
+    rows_ref[3 * rows_d : 3 * rows_d + tall, :] = side[:tall, :lanes] + half_ref[tall:, :]
+    spot = lax.broadcasted_iota(jnp.int32, (1, lanes), 1)
+    times = where_ref[5].astype(F32)
+    plans = where_ref[6].astype(F32)
+    rows_ref[3 * rows_d + tall : 3 * rows_d + tall + 1, :] = jnp.where(
+        spot == 0, times, jnp.where(spot == 1, plans, 0.0)
+    )
+    main_ref[...] = rows_ref[...][: main_ref.shape[0], :].astype(BF16)
+
+
 def local(
     start_noise,
     position,
@@ -413,45 +485,46 @@
     frame, zlo, zhi, core = (lax.axis_index(a) for a in ("frame", "zlo", "zhi", "head"))
     step = zhi * zlo_n + zlo
 
-    proj_mine = chosen([w_proj[:, f * cols : (f + 1) * cols] for f in range(frames)], frame)
-    final_mine = lax.dynamic_slice_in_dim(w_final, step * rows_d, rows_d, 1)
-    mix = jnp.dot(final_mine, proj_mine, preferred_element_type=F32)
-    mix = lax.all_to_all(mix.reshape(zlo_n, lat // zlo_n, cols), "zlo", 0, 0, tiled=True)
-    mix = jnp.sum(mix, axis=0).T.astype(BF16)
-
-    qkv_mine = chosen([w_qkv[:, :, f * cols : (f + 1) * cols] for f in range(frames)], frame)
-    main = [qkv_mine[:, k, :lanes] for k in range(3)]
-    rest = jnp.concatenate([qkv_mine[:, k, lanes:] for k in range(3)], axis=1)
+    where = jnp.concatenate(
+        [jnp.stack([zhi, frame, zlo, core, step]).astype(jnp.int32), time_index, sched_index]
+    )
     tall = rows_d // 2
+    extra = cols - lanes
     pieces = cols // tall
-    side = jnp.concatenate(
-        [rest[:tall], rest[tall:]] + [mix[g * tall : (g + 1) * tall] for g in range(pieces)], axis=1
-    )
-    index_row = jnp.concatenate([time_index, sched_index]).astype(BF16)
-    index_row = jnp.pad(index_row, (0, lanes - 2))[None]
-    payload = jnp.concatenate(main + [side, index_row], axis=0)
+    payload_rows = 3 * rows_d + tall + 1
+    mix, frame_load, payload = smem_first(
+        functools.partial(pack_body, extra),
+        (
+            jax.ShapeDtypeStruct((zlo_n, lat // zlo_n, cols), F32),
+            jax.ShapeDtypeStruct((frames, row_count + lat, model), BF16),
+            jax.ShapeDtypeStruct((payload_rows, lanes), BF16),
+        ),
+        where,
+        w_qkv.transpose(1, 0, 2),
+        w_proj,
+        w_final,
+        start_noise,
+        position,
+        scratch=(pltpu.VMEM((payload_rows + 1, lanes), F32), pltpu.VMEM((rows_d, lanes), F32)),
+        name="pack",
+    )
+
+    mix = jnp.sum(lax.all_to_all(mix, "zlo", 0, 0, tiled=True), axis=0)
+    mix = mix.reshape(lat // zlo_n, pieces, tall).transpose(2, 1, 0).reshape(tall, -1)
+    payload = payload + jnp.pad(
+        mix.astype(BF16), ((3 * rows_d, 1), (6 * extra, lanes - 6 * extra - mix.shape[1]))
+    )
+
+    frame_all = lax.all_to_all(frame_load, "frame", 0, 0, tiled=True)
+
     gathered = lax.all_gather(payload, STEP, axis=0)
 
-    noise_rows = jnp.pad(start_noise.astype(BF16), ((0, 0), (0, model - row_count)))
-    frame_load = jnp.concatenate([position, noise_rows], axis=0)
-    frame_all = lax.all_to_all(
-        jnp.broadcast_to(frame_load[None], (frames, *frame_load.shape)), "frame", 0, 0, tiled=True
-    )
     sides = gathered[:, 3 * rows_d : 3 * rows_d + tall]
-    extra = cols - lanes
-    w_rest = jnp.concatenate([sides[:, :, : 3 * extra], sides[:, :, 3 * extra : 6 * extra]], axis=1)
-    w_rest = jnp.pad(w_rest, ((0, 0), (0, 0), (0, lanes - 3 * extra)))
-    w_all = jnp.concatenate(
-        [gathered[:, k * rows_d : (k + 1) * rows_d] for k in range(3)] + [w_rest], axis=2
-    ).reshape(step_n * rows_d, 4 * lanes)
     part = lat // zlo_n
     mixes = sides[:, :, 6 * extra :].astype(F32).reshape(zhi_n, zlo_n, tall, pieces, part)
     mixes = jnp.sum(mixes, axis=0).transpose(0, 3, 2, 1).reshape(lat, cols)
     mix_hi = lax.reduce_precision(mixes, 8, 7)
     wfp = jnp.concatenate([mix_hi, mixes - mix_hi], axis=0).astype(BF16)
-    index_rows = gathered[:, 3 * rows_d + tall].astype(F32)
-
-    where = jnp.stack([zhi, frame, zlo, core]).astype(jnp.int32)
     bext, a_all, c_all, base, fblk, coef, noise, states, x = smem_first(
         functools.partial(prep_body, lat, cores, extra),
         (
@@ -466,18 +539,22 @@
             jax.ShapeDtypeStruct((tokens, lanes), BF16),
         ),
         where,
-        w_all,
+        gathered,
         frame_all,
         position,
         start_noise,
-        index_rows,
         time_table,
         norm_gain[None],
         coef_keep[None],
         coef_noise[None],
         w_in,
         w_final,
-        scratch=(pltpu.VMEM((step_n, model), F32), pltpu.VMEM((row_count, lanes), F32)),
+        scratch=(
+            pltpu.VMEM((step_n, model), F32),
+            pltpu.VMEM((row_count, lanes), F32),
+            pltpu.VMEM((step_n * rows_d, 4 * lanes), F32),
+            pltpu.VMEM((step_n, lanes), F32),
+        ),
         name="prep",
     )
 

time: 265 us -> 262 us (0.989)
  other arithmetic: 4.83 us -> 0.28 us
  waiting for transfers between devices: 0.01 us -> 3.77 us
    unnamed x17 -> x25, local copies, waits for them, and re-layouts: 0.35 us -> 4.49 us
    all_to_all x2, waiting for transfers between devices: 0.01 us -> 3.77 us  [the longest x1 3.76 us: local(): mix = jnp.sum(lax.all_to_all(mix, 'zlo', 0, 0, tiled=True), axis=0)]
    reshape x2 -> x0, local copies, waits for them, and re-layouts: 2.82 us -> none  [the longest x1 2.21 us: local(): w_all = jnp.concatenate([gathered[:, k * rows_d:(k + 1) * rows_d] for k i...]
    all_gather x1, blocking collectives: 84.4 us -> 81.7 us  [local(): gathered = lax.all_gather(payload, STEP, axis=0)]
    pallas_call x3 -> x4, Pallas kernels: 5.95 us -> 8.16 us  [smem_first(): pl.pallas_call(body, out_shape=out_shape, in_specs=[pl.BlockSpec(memory_s...]
  transfers between devices with their start and end apart: 2 -> 2, of which waited for: 0 -> 1; matrix products, arithmetic and copies ran while one was open for 3% -> 1% of each run, Pallas kernels for 0% -> 0%
where the time goes in v3:
time: 262 us; the launch traced here: 261 us
  blocking collectives  195 us (74%)
  Pallas kernels  40.1 us (15%)
  starting transfers between devices  13.3 us (5%)
  local copies, waits for them, and re-layouts  6.2 us (2%)
  waiting for transfers between devices  3.77 us (1%)
    all_gather x1, blocking collectives, local(): gathered = lax.all_gather(payload, STEP, axis=0)  81.7 us
    all_to_all x4, blocking collectives, local(): lax.all_to_all(part_eps.reshape(members, mine, lanes), HOOD, 0, 0, tiled=...  64.9 us
    all_to_all x3, blocking collectives, local(): x = lax.all_to_all(send, HOOD, 0, 0, tiled=True).reshape(tokens, lanes)  36.5 us
    pallas_call x7, Pallas kernels, vmem_call(): pl.pallas_call(body, out_shape=out_shape, in_specs=[spec] * len(args), ou...  31.9 us
    all_to_all x1, blocking collectives, local(): ended = lax.all_to_all(send, HOOD, 0, 0, tiled=True)  12.2 us
    all_to_all x1, starting transfers between devices, local(): mix = jnp.sum(lax.all_to_all(mix, 'zlo', 0, 0, tiled=True), axis=0)  9.02 us
    pallas_call x4, Pallas kernels, smem_first(): pl.pallas_call(body, out_shape=out_shape, in_specs=[pl.BlockSpec(memory_s...  8.16 us
  transfers between devices with their start and end apart: 2, of which 1 were waited for; matrix products, arithmetic and copies ran while one was open for 1% of the time, Pallas kernels for 0%

profile of v3, /device:TPU:33, one launch (start us, length us, event | category | flops | bytes accessed | tf_op | source)
XLA Modules:
  0.0 261.1 jit_solution(12346270781328615906)
XLA Ops:
  1.9 0.1 concatenate.7.where_ref
  2.0 1.0 copy-done
  3.0 0.9 copy-done.3
  3.9 0.8 copy-done.4
  4.7 0.8 copy-done.6
  5.5 0.7 copy-done.8
  6.2 2.3 pack.1
  8.5 9.0 %all-to-all-start = ((f32[4,4,144]{2,1,0:T(4,128)}), f32[4,4,144]{2,1,0:T(4,128)S(1)}, u32[]{:S(2)}, u32[]{:S(2)}) async-start(f32[4,4,144]{2,1,0:T(4,128)} %get-tuple-element.26), calls=%async_computation | async-start | bytes 32768 | tf_op jit(solution)/shard_map/all_to_all | solution.py:512
  17.5 0.7 broadcast_in_dim.12.gain_ref
  18.2 3.8 %all-to-all-done = f32[4,4,144]{2,1,0:T(4,128)S(1)} async-done(((f32[4,4,144]{2,1,0:T(4,128)}), f32[4,4,144]{2,1,0:T(4,128)S(1)}, u32[]{:S(2)}, u32[]{:S(2)}) %all-to-all-start) | async-done | bytes 9248 | tf_op jit(solution)/shard_map/all_to_all | solution.py:512
  22.0 4.3 %all-to-all-start.1 = ((bf16[4,144,1152]{2,1,0:T(8,128)(2,1)}), bf16[4,144,1152]{2,1,0:T(8,128)(2,1)S(1)}, u32[]{:S(2)}, u32[]{:S(2)}) async-start(bf16[4,144,1152]{2,1,0:T(8,128)(2,1)} %get-tuple-element.27), calls=%async_computation.1 | async-start | bytes 2654208 | tf_op jit(solution)/shard_map/all_to_all | solution.py:518
  26.3 0.1 convert_element_type.17
  26.4 0.0 copy-start.2
  26.4 0.0 copy-start.5
  26.4 0.0 copy-start.7
  26.4 0.0 copy-start.9
  26.4 0.0 copy-start.10
  26.4 0.0 copy-start.11
  26.5 0.1 copy.18
  26.6 0.1 add_bitcast_fusion
  26.6 81.7 %all-gather.1.got_ref = bf16[32,127,128]{2,1,0:T(8,128)(2,1)S(1)} all-gather(bf16[1,127,128]{2,1,0:T(8,128)(2,1)S(1)} %add_bitcast_fusion), channel_id=2, replica_groups=mesh['parts'=2,'zhi'=8,'zlo'=4,'frame'=4,'head'=2] {'zhi','zlo'}, dimensions={0}, use_global_device_ids=true | all-gather | bytes 1072896 | tf_op jit(solution)/shard_map/all_gather | solution.py:520
  108.3 0.1 slice.10
  108.5 0.3 copy.21
  108.8 0.2 convert_reduce_fusion
  109.0 0.1 reshape.40
  109.1 0.0 all-to-all-done.1.all_ref
  109.1 0.0 copy-done.1
  109.1 0.0 copy-done.2
  109.1 0.0 copy-done.5
  109.1 3.3 %prep.1 = (f32[448,512]{1,0:T(8,128)S(1)}, bf16[448,128]{1,0:T(8,128)(2,1)S(1)}, f32[8,512]{1,0:T(8,128)S(1)}, f32[4,16,128]{2,1,0:T(8,128)S(1)}, bf16[384,128]{...) custom-call(s32[7]{0:T(128)S(1)} %concatenate.7.where_ref, ...), custom_call_target="tpu_custom_call" | custom-call | tf_op jit(solution)/shard_map/prep/pallas_call | solution.py:246
  112.4 7.5 %eps_part.4 = bf16[512,128]{1,0:T(8,128)(2,1)S(1)} custom-call(bf16[512,128]{1,0:T(8,128)(2,1)S(1)} %get-tuple-element.28.x_ref, f32[448,512]{1,0:T(8,128)S(1)} %get-tuple-element.29.bext_ref, bf16[448,128]{1,0:T(8,128)(2,1)S(1)} %get-tuple-element.30.a_ref, f32[8,512]{1,0:T(8,128)S(1)} %get-tuple-element.31.c_ref, bf16[32,144]{1,0:T(8,128)(2,1)S(1)} %pad_maximum_fusion.wfp_ref), custom_call_target="tpu_custom_call" | custom-call | flops 1577058304 | tf_op jit(solution)/shard_map/eps_part/pallas_call | solution.py:31
  120.0 28.4 %all_to_all.50.got_ref = bf16[32,16,128]{2,1,0:T(8,128)(2,1)S(1)} all-to-all(bf16[32,16,128]{2,1,0:T(8,128)(2,1)S(1)} %bitcast.30), channel_id=1, replica_groups=mesh['parts'=2,'zhi'=8,'zlo'=4,'frame'=4,'head'=2] {'frame','zlo','head'}, dimensions={0} | all-to-all | bytes 262144 | tf_op jit(solution)/shard_map/all_to_all | solution.py:564
  148.4 0.6 advance.3
  149.0 12.2 %all_to_all.51 = bf16[32,16,128]{2,1,0:T(8,128)(2,1)S(1)} all-to-all(bf16[32,16,128]{2,1,0:T(8,128)(2,1)S(1)} %get-tuple-element.37), channel_id=1, replica_groups=mesh['parts'=2,'zhi'=8,'zlo'=4,'frame'=4,'head'=2] {'frame','zlo','head'}, dimensions={0} | all-to-all | bytes 262144 | tf_op jit(solution)/shard_map/all_to_all | solution.py:582
  161.2 7.5 %eps_part.5 = bf16[512,128]{1,0:T(8,128)(2,1)S(1)} custom-call(bf16[512,128]{1,0:T(8,128)(2,1)S(1)} %bitcast.31, f32[448,512]{1,0:T(8,128)S(1)} %get-tuple-element.29.bext_ref, bf16[448,128]{1,0:T(8,128)(2,1)S(1)} %get-tuple-element.30.a_ref, f32[8,512]{1,0:T(8,128)S(1)} %get-tuple-element.31.c_ref, bf16[32,144]{1,0:T(8,128)(2,1)S(1)} %pad_maximum_fusion.wfp_ref), custom_call_target="tpu_custom_call" | custom-call | flops 1577058304 | tf_op jit(solution)/shard_map/eps_part/pallas_call | solution.py:31
  168.7 12.2 %all_to_all.52.got_ref = bf16[32,16,128]{2,1,0:T(8,128)(2,1)S(1)} all-to-all(bf16[32,16,128]{2,1,0:T(8,128)(2,1)S(1)} %bitcast.32), channel_id=1, replica_groups=mesh['parts'=2,'zhi'=8,'zlo'=4,'frame'=4,'head'=2] {'frame','zlo','head'}, dimensions={0} | all-to-all | bytes 262144 | tf_op jit(solution)/shard_map/all_to_all | solution.py:564
  180.9 0.6 advance.4
  181.5 12.2 %all_to_all.53 = bf16[32,16,128]{2,1,0:T(8,128)(2,1)S(1)} all-to-all(bf16[32,16,128]{2,1,0:T(8,128)(2,1)S(1)} %get-tuple-element.39), channel_id=1, replica_groups=mesh['parts'=2,'zhi'=8,'zlo'=4,'frame'=4,'head'=2] {'frame','zlo','head'}, dimensions={0} | all-to-all | bytes 262144 | tf_op jit(solution)/shard_map/all_to_all | solution.py:582
  193.6 7.5 %eps_part.6 = bf16[512,128]{1,0:T(8,128)(2,1)S(1)} custom-call(bf16[512,128]{1,0:T(8,128)(2,1)S(1)} %bitcast.33, f32[448,512]{1,0:T(8,128)S(1)} %get-tuple-element.29.bext_ref, bf16[448,128]{1,0:T(8,128)(2,1)S(1)} %get-tuple-element.30.a_ref, f32[8,512]{1,0:T(8,128)S(1)} %get-tuple-element.31.c_ref, bf16[32,144]{1,0:T(8,128)(2,1)S(1)} %pad_maximum_fusion.wfp_ref), custom_call_target="tpu_custom_call" | custom-call | flops 1577058304 | tf_op jit(solution)/shard_map/eps_part/pallas_call | solution.py:31
  201.2 12.2 %all_to_all.54.got_ref = bf16[32,16,128]{2,1,0:T(8,128)(2,1)S(1)} all-to-all(bf16[32,16,128]{2,1,0:T(8,128)(2,1)S(1)} %bitcast.34), channel_id=1, replica_groups=mesh['parts'=2,'zhi'=8,'zlo'=4,'frame'=4,'head'=2] {'frame','zlo','head'}, dimensions={0} | all-to-all | bytes 262144 | tf_op jit(solution)/shard_map/all_to_all | solution.py:564
  213.4 0.6 advance.5
  214.0 12.2 %all_to_all.55 = bf16[32,16,128]{2,1,0:T(8,128)(2,1)S(1)} all-to-all(bf16[32,16,128]{2,1,0:T(8,128)(2,1)S(1)} %get-tuple-element.41), channel_id=1, replica_groups=mesh['parts'=2,'zhi'=8,'zlo'=4,'frame'=4,'head'=2] {'frame','zlo','head'}, dimensions={0} | all-to-all | bytes 262144 | tf_op jit(solution)/shard_map/all_to_all | solution.py:582
  226.1 7.5 %eps_part.7 = bf16[512,128]{1,0:T(8,128)(2,1)S(1)} custom-call(bf16[512,128]{1,0:T(8,128)(2,1)S(1)} %bitcast.28, f32[448,512]{1,0:T(8,128)S(1)} %get-tuple-element.29.bext_ref, bf16[448,128]{1,0:T(8,128)(2,1)S(1)} %get-tuple-element.30.a_ref, f32[8,512]{1,0:T(8,128)S(1)} %get-tuple-element.31.c_ref, bf16[32,144]{1,0:T(8,128)(2,1)S(1)} %pad_maximum_fusion.wfp_ref), custom_call_target="tpu_custom_call" | custom-call | flops 1577058304 | tf_op jit(solution)/shard_map/eps_part/pallas_call | solution.py:31
  233.7 12.2 %all_to_all.56.got_ref = bf16[32,16,128]{2,1,0:T(8,128)(2,1)S(1)} all-to-all(bf16[32,16,128]{2,1,0:T(8,128)(2,1)S(1)} %bitcast.29), channel_id=1, replica_groups=mesh['parts'=2,'zhi'=8,'zlo'=4,'frame'=4,'head'=2] {'frame','zlo','head'}, dimensions={0} | all-to-all | bytes 262144 | tf_op jit(solution)/shard_map/all_to_all | solution.py:564
  245.8 1.3 last.1
  247.1 12.2 %all_to_all.57.got_ref = f32[32,8,128]{2,1,0:T(8,128)S(1)} all-to-all(f32[32,8,128]{2,1,0:T(8,128)S(1)} %last.1), channel_id=1, replica_groups=mesh['parts'=2,'zhi'=8,'zlo'=4,'frame'=4,'head'=2] {'frame','zlo','head'}, dimensions={0} | all-to-all | bytes 262144 | tf_op jit(solution)/shard_map/all_to_all | solution.py:597
  259.3 1.3 end.1
  260.5 0.5 slice_bitcast_fusion
  (15 shorter events, 0.1 us)
Async XLA Ops:
  2.0 1.0 copy-start
  3.0 0.9 copy-start.3
  3.9 0.8 copy-start.4
  4.7 0.8 copy-start.6
  5.5 0.7 copy-start.8
  8.5 13.5 %all-to-all-start = ((f32[4,4,144]{2,1,0:T(4,128)}), f32[4,4,144]{2,1,0:T(4,128)S(1)}, u32[]{:S(2)}, u32[]{:S(2)}) async-start(f32[4,4,144]{2,1,0:T(4,128)} %get-tuple-element.26), calls=%async_computation | async-start | bytes 32768 | tf_op jit(solution)/shard_map/all_to_all | solution.py:512
  22.0 87.1 %all-to-all-start.1 = ((bf16[4,144,1152]{2,1,0:T(8,128)(2,1)}), bf16[4,144,1152]{2,1,0:T(8,128)(2,1)S(1)}, u32[]{:S(2)}, u32[]{:S(2)}) async-start(bf16[4,144,1152]{2,1,0:T(8,128)(2,1)} %get-tuple-element.27), calls=%async_computation.1 | async-start | bytes 2654208 | tf_op jit(solution)/shard_map/all_to_all | solution.py:518
  26.4 82.7 %copy-start.1 = (bf16[128,1152]{1,0:T(8,128)(2,1)S(1)}, bf16[128,1152]{1,0:T(8,128)(2,1)}, u32[]{:S(2)}) copy-start(bf16[128,1152]{1,0:T(8,128)(2,1)} %position_ref.3) | copy-start | bytes 884740
  26.4 82.7 %copy-start.2 = (bf16[128,1152]{1,0:T(8,128)(2,1)S(1)}, bf16[128,1152]{1,0:T(8,128)(2,1)}, u32[]{:S(2)}) copy-start(bf16[128,1152]{1,0:T(8,128)(2,1)} %table_ref.1) | copy-start | bytes 884740
  26.4 82.7 %copy-start.5 = (bf16[16,1152]{1,0:T(8,128)(2,1)S(1)}, bf16[16,1152]{1,0:T(8,128)(2,1)}, u32[]{:S(2)}) copy-start(bf16[16,1152]{1,0:T(8,128)(2,1)} %final_ref.3) | copy-start | bytes 110596
  26.4 82.7 %copy-start.7 = (bf16[16,1152]{1,0:T(8,128)(2,1)S(1)}, bf16[16,1152]{1,0:T(8,128)(2,1)}, u32[]{:S(2)}) copy-start(bf16[16,1152]{1,0:T(8,128)(2,1)} %w_in_ref.1) | copy-start | bytes 110596
  26.4 82.7 %copy-start.9 = (f32[16,128]{1,0:T(8,128)S(1)}, f32[16,128]{1,0:T(8,128)}, u32[]{:S(2)}) copy-start(f32[16,128]{1,0:T(8,128)} %start_ref.3) | copy-start | bytes 24580
  26.4 82.7 %copy-start.10 = (f32[128]{0:T(128)S(1)}, f32[128]{0:T(128)}, u32[]{:S(2)}) copy-start(f32[128]{0:T(128)} %param.17) | copy-start | bytes 1540
  26.4 82.7 %copy-start.11 = (f32[128]{0:T(128)S(1)}, f32[128]{0:T(128)}, u32[]{:S(2)}) copy-start(f32[128]{0:T(128)} %param.18) | copy-start | bytes 1540

commit v4 on v3

--- a/solution.py
+++ b/solution.py
@@ -231,7 +231,9 @@
         everyone = everyone + got_ref[member]
     slot = lax.rem(zlo + 1, groups)
     sums = pltpu.roll(everyone, lax.rem(lanes - slot * lat, lanes), 1)
-    norm_ref[...] = jnp.sqrt(sums / cells + 1e-06)
+    norms = jnp.sqrt(sums[:1] / cells + 1e-06)
+    for at in range(ITERS):
+        norm_ref[at] = norms[0, at]
     rows = []
     back = lax.rem(lanes - zlo * lat, lanes)
     for own in range(groups * cores):
@@ -241,15 +243,18 @@
     traj_ref[...] = jnp.concatenate(rows, axis=0).T[:lat, :]
 
 
-def smem_first(body, out_shape, where, *args, scratch=(), name=None):
+def smem_first(body, out_shape, where, *args, scratch=(), grant=GRANT, scalars=(), name=None):
     spec = pl.BlockSpec(memory_space=pltpu.VMEM)
+    out_specs = jax.tree.map(lambda _: spec, out_shape)
+    for at in scalars:
+        out_specs = (*out_specs[:at], pl.BlockSpec(memory_space=pltpu.SMEM), *out_specs[at + 1 :])
     return pl.pallas_call(
         body,
         out_shape=out_shape,
         in_specs=[pl.BlockSpec(memory_space=pltpu.SMEM)] + [spec] * len(args),
-        out_specs=jax.tree.map(lambda _: spec, out_shape),
+        out_specs=out_specs,
         scratch_shapes=list(scratch),
-        compiler_params=pltpu.CompilerParams(vmem_limit_bytes=GRANT),
+        compiler_params=pltpu.CompilerParams(vmem_limit_bytes=grant),
         name=name,
     )(where, *args)
 
@@ -352,7 +357,7 @@
     blank = jnp.zeros((lanes - 3 * (lat + steps), model), F32)
     thin = jnp.concatenate([w_in, w_in, w_in, temb, temb, temb, blank], axis=0)
     thin_bf = thin.astype(BF16)
-    gain = gain_ref[...]
+    gain = jnp.concatenate([gain_ref[at : at + 1] for at in range(model // lanes)], axis=1)
     w = w_ref[...].astype(BF16)
     thin_hi, thin_lo = split_two(thin * gain)
     linear = jnp.dot(thin_hi, w, preferred_element_type=F32) + jnp.dot(
@@ -506,6 +511,7 @@
         start_noise,
         position,
         scratch=(pltpu.VMEM((payload_rows + 1, lanes), F32), pltpu.VMEM((rows_d, lanes), F32)),
+        grant=None,
         name="pack",
     )
 
@@ -544,7 +550,7 @@
         position,
         start_noise,
         time_table,
-        norm_gain[None],
+        norm_gain.reshape(-1, lanes),
         coef_keep[None],
         coef_noise[None],
         w_in,
@@ -599,13 +605,14 @@
         functools.partial(end_body, lat, frames, cores, float(step_n * lat * tokens)),
         (
             jax.ShapeDtypeStruct((lat, row_count), F32),
-            jax.ShapeDtypeStruct((mine // 2, lanes), F32),
+            jax.ShapeDtypeStruct((ITERS,), F32),
         ),
         where,
         ended,
+        scalars=(1,),
         name="end",
     )
-    return trajectory[None], norms[0, :ITERS]
+    return trajectory[None], norms
 
 
 def solution(mesh):

time: 262 us -> 258 us (0.985)
  blocking collectives: 195 us -> 209 us
  starting transfers between devices: 13.3 us -> 4.43 us
  local copies, waits for them, and re-layouts: 6.2 us -> 1.4 us
  waiting for transfers between devices: 3.77 us -> 0.01 us
    all_to_all x0 -> x1, blocking collectives: none -> 13.5 us  [local(): mix = jnp.sum(lax.all_to_all(mix, 'zlo', 0, 0, tiled=True), axis=0)]
    all_to_all x1 -> x0, starting transfers between devices: 9.02 us -> none  [local(): mix = jnp.sum(lax.all_to_all(mix, 'zlo', 0, 0, tiled=True), axis=0)]
    unnamed x25 -> x21, local copies, waits for them, and re-layouts: 4.49 us -> 0.36 us
    all_to_all x1 -> x0, waiting for transfers between devices: 3.76 us -> none  [local(): mix = jnp.sum(lax.all_to_all(mix, 'zlo', 0, 0, tiled=True), axis=0)]
  transfers between devices with their start and end apart: 2 -> 1, of which waited for: 1 -> 0; matrix products, arithmetic and copies ran while one was open for 1% -> 0% of each run, Pallas kernels for 0% -> 0%
where the time goes in v4:
time: 258 us
  blocking collectives  209 us (81%)
  Pallas kernels  40.7 us (16%)
  starting transfers between devices  4.43 us (2%)
    all_gather x1, blocking collectives, local(): gathered = lax.all_gather(payload, STEP, axis=0)  81.7 us
    all_to_all x4, blocking collectives, local(): lax.all_to_all(part_eps.reshape(members, mine, lanes), HOOD, 0, 0, tiled=...  64.9 us
    all_to_all x3, blocking collectives, local(): x = lax.all_to_all(send, HOOD, 0, 0, tiled=True).reshape(tokens, lanes)  36.5 us
    pallas_call x7, Pallas kernels, vmem_call(): pl.pallas_call(body, out_shape=out_shape, in_specs=[spec] * len(args), ou...  31.7 us
    all_to_all x1, blocking collectives, local(): mix = jnp.sum(lax.all_to_all(mix, 'zlo', 0, 0, tiled=True), axis=0)  13.5 us
    all_to_all x1, blocking collectives, local(): ended = lax.all_to_all(send, HOOD, 0, 0, tiled=True)  12.2 us
    pallas_call x4, Pallas kernels, smem_first(): pl.pallas_call(body, out_shape=out_shape, in_specs=[pl.BlockSpec(memory_s...  8.91 us
  transfers between devices with their start and end apart: 1, of which 0 were waited for; matrix products, arithmetic and copies ran while one was open for 0% of the time, Pallas kernels for 0%

profile of v4, /device:TPU:33, one launch (start us, length us, event | category | flops | bytes accessed | tf_op | source)
XLA Modules:
  0.0 257.8 jit_solution(18253373836997359997)
XLA Ops:
  1.9 0.6 concatenate.7.where_ref
  2.6 2.9 %pack.1 = (f32[4,4,144]{2,1,0:T(4,128)}, bf16[4,144,1152]{2,1,0:T(8,128)(2,1)}, bf16[127,128]{1,0:T(8,128)(2,1)}) custom-call(s32[7]{0:T(128)} %concatenate.7.where_ref, bf16[3,36,576]{2,1,0:T(8,128)(2,1)} %bitcast.38, bf16[36,576]{1,0:T(8,128)(2,1)} %proj_ref.1, bf16[16,1152]{1,0:T(8,128)(2,1)} %final_ref.3, f32[16,128]{1,0:T(8,128)} %start_ref.3, ...), custom_call_target="tpu_custom_call" | custom-call | tf_op jit(solution)/shard_map/pack/pallas_call | solution.py:251
  5.4 13.5 %all_to_all.50 = f32[4,4,144]{2,1,0:T(4,128)S(1)} all-to-all(f32[4,4,144]{2,1,0:T(4,128)} %get-tuple-element.26), channel_id=1, replica_groups=mesh['parts'=2,'zhi'=8,'zlo'=4,'frame'=4,'head'=2] {'zlo'}, dimensions={0} | all-to-all | bytes 18432 | tf_op jit(solution)/shard_map/all_to_all | solution.py:518
  18.9 4.4 %all-to-all-start.1 = ((bf16[4,144,1152]{2,1,0:T(8,128)(2,1)}), bf16[4,144,1152]{2,1,0:T(8,128)(2,1)S(1)}, u32[]{:S(2)}, u32[]{:S(2)}) async-start(bf16[4,144,1152]{2,1,0:T(8,128)(2,1)} %get-tuple-element.27), calls=%async_computation.1 | async-start | bytes 2654208 | tf_op jit(solution)/shard_map/all_to_all | solution.py:524
  23.4 0.1 convert_element_type.17
  23.5 0.0 copy-start.1
  23.5 0.0 copy-start.2
  23.5 0.0 copy-start.3
  23.5 0.0 copy-start.4
  23.5 0.0 copy-start.5
  23.5 0.0 copy-start.6
  23.5 0.0 copy-start.7
  23.6 0.0 copy-start.8
  23.6 0.1 copy.18
  23.7 0.0 copy-done.9
  23.7 0.1 add_bitcast_fusion
  23.8 81.7 %all-gather.1.got_ref = bf16[32,127,128]{2,1,0:T(8,128)(2,1)S(1)} all-gather(bf16[1,127,128]{2,1,0:T(8,128)(2,1)S(1)} %add_bitcast_fusion), channel_id=2, replica_groups=mesh['parts'=2,'zhi'=8,'zlo'=4,'frame'=4,'head'=2] {'zhi','zlo'}, dimensions={0}, use_global_device_ids=true | all-gather | bytes 1072896 | tf_op jit(solution)/shard_map/all_gather | solution.py:526
  105.5 0.1 slice.6
  105.6 0.3 copy.21
  105.9 0.2 convert_reduce_fusion
  106.1 0.1 reshape.44
  106.2 0.0 all-to-all-done.1.all_ref
  106.2 0.0 copy-done
  106.2 0.0 copy-done.1
  106.2 0.0 copy-done.2
  106.2 0.0 copy-done.3
  106.2 0.0 copy-done.4
  106.2 0.0 copy-done.5
  106.2 0.0 copy-done.6
  106.3 0.0 copy-done.7
  106.3 3.4 %prep.1 = (f32[448,512]{1,0:T(8,128)S(1)}, bf16[448,128]{1,0:T(8,128)(2,1)S(1)}, f32[8,512]{1,0:T(8,128)S(1)}, f32[4,16,128]{2,1,0:T(8,128)S(1)}, bf16[384,128]{...) custom-call(s32[7]{0:T(128)S(1)} %copy-done.5, ...), custom_call_target="tpu_custom_call" | custom-call | tf_op jit(solution)/shard_map/prep/pallas_call | solution.py:251
  109.7 7.5 %eps_part.4 = bf16[512,128]{1,0:T(8,128)(2,1)S(1)} custom-call(bf16[512,128]{1,0:T(8,128)(2,1)S(1)} %get-tuple-element.28.x_ref, f32[448,512]{1,0:T(8,128)S(1)} %get-tuple-element.29.bext_ref, bf16[448,128]{1,0:T(8,128)(2,1)S(1)} %get-tuple-element.30.a_ref, f32[8,512]{1,0:T(8,128)S(1)} %get-tuple-element.31.c_ref, bf16[32,144]{1,0:T(8,128)(2,1)S(1)} %pad_maximum_fusion.wfp_ref), custom_call_target="tpu_custom_call" | custom-call | flops 1577058304 | tf_op jit(solution)/shard_map/eps_part/pallas_call | solution.py:31
  117.2 28.4 %all_to_all.51.got_ref = bf16[32,16,128]{2,1,0:T(8,128)(2,1)S(1)} all-to-all(bf16[32,16,128]{2,1,0:T(8,128)(2,1)S(1)} %bitcast.28), channel_id=1, replica_groups=mesh['parts'=2,'zhi'=8,'zlo'=4,'frame'=4,'head'=2] {'frame','zlo','head'}, dimensions={0} | all-to-all | bytes 262144 | tf_op jit(solution)/shard_map/all_to_all | solution.py:570
  145.6 0.6 advance.3
  146.2 12.2 %all_to_all.52 = bf16[32,16,128]{2,1,0:T(8,128)(2,1)S(1)} all-to-all(bf16[32,16,128]{2,1,0:T(8,128)(2,1)S(1)} %get-tuple-element.37), channel_id=1, replica_groups=mesh['parts'=2,'zhi'=8,'zlo'=4,'frame'=4,'head'=2] {'frame','zlo','head'}, dimensions={0} | all-to-all | bytes 262144 | tf_op jit(solution)/shard_map/all_to_all | solution.py:588
  158.3 7.5 %eps_part.5 = bf16[512,128]{1,0:T(8,128)(2,1)S(1)} custom-call(bf16[512,128]{1,0:T(8,128)(2,1)S(1)} %bitcast.29, f32[448,512]{1,0:T(8,128)S(1)} %get-tuple-element.29.bext_ref, bf16[448,128]{1,0:T(8,128)(2,1)S(1)} %get-tuple-element.30.a_ref, f32[8,512]{1,0:T(8,128)S(1)} %get-tuple-element.31.c_ref, bf16[32,144]{1,0:T(8,128)(2,1)S(1)} %pad_maximum_fusion.wfp_ref), custom_call_target="tpu_custom_call" | custom-call | flops 1577058304 | tf_op jit(solution)/shard_map/eps_part/pallas_call | solution.py:31
  165.8 12.1 %all_to_all.53.got_ref = bf16[32,16,128]{2,1,0:T(8,128)(2,1)S(1)} all-to-all(bf16[32,16,128]{2,1,0:T(8,128)(2,1)S(1)} %bitcast.30), channel_id=1, replica_groups=mesh['parts'=2,'zhi'=8,'zlo'=4,'frame'=4,'head'=2] {'frame','zlo','head'}, dimensions={0} | all-to-all | bytes 262144 | tf_op jit(solution)/shard_map/all_to_all | solution.py:570
  178.0 0.6 advance.4
  178.6 12.2 %all_to_all.54 = bf16[32,16,128]{2,1,0:T(8,128)(2,1)S(1)} all-to-all(bf16[32,16,128]{2,1,0:T(8,128)(2,1)S(1)} %get-tuple-element.39), channel_id=1, replica_groups=mesh['parts'=2,'zhi'=8,'zlo'=4,'frame'=4,'head'=2] {'frame','zlo','head'}, dimensions={0} | all-to-all | bytes 262144 | tf_op jit(solution)/shard_map/all_to_all | solution.py:588
  190.8 7.5 %eps_part.6 = bf16[512,128]{1,0:T(8,128)(2,1)S(1)} custom-call(bf16[512,128]{1,0:T(8,128)(2,1)S(1)} %bitcast.31, f32[448,512]{1,0:T(8,128)S(1)} %get-tuple-element.29.bext_ref, bf16[448,128]{1,0:T(8,128)(2,1)S(1)} %get-tuple-element.30.a_ref, f32[8,512]{1,0:T(8,128)S(1)} %get-tuple-element.31.c_ref, bf16[32,144]{1,0:T(8,128)(2,1)S(1)} %pad_maximum_fusion.wfp_ref), custom_call_target="tpu_custom_call" | custom-call | flops 1577058304 | tf_op jit(solution)/shard_map/eps_part/pallas_call | solution.py:31
  198.2 12.2 %all_to_all.55.got_ref = bf16[32,16,128]{2,1,0:T(8,128)(2,1)S(1)} all-to-all(bf16[32,16,128]{2,1,0:T(8,128)(2,1)S(1)} %bitcast.32), channel_id=1, replica_groups=mesh['parts'=2,'zhi'=8,'zlo'=4,'frame'=4,'head'=2] {'frame','zlo','head'}, dimensions={0} | all-to-all | bytes 262144 | tf_op jit(solution)/shard_map/all_to_all | solution.py:570
  210.4 0.6 advance.5
  211.0 12.2 %all_to_all.56 = bf16[32,16,128]{2,1,0:T(8,128)(2,1)S(1)} all-to-all(bf16[32,16,128]{2,1,0:T(8,128)(2,1)S(1)} %get-tuple-element.41), channel_id=1, replica_groups=mesh['parts'=2,'zhi'=8,'zlo'=4,'frame'=4,'head'=2] {'frame','zlo','head'}, dimensions={0} | all-to-all | bytes 262144 | tf_op jit(solution)/shard_map/all_to_all | solution.py:588
  223.2 7.5 %eps_part.7 = bf16[512,128]{1,0:T(8,128)(2,1)S(1)} custom-call(bf16[512,128]{1,0:T(8,128)(2,1)S(1)} %bitcast.26, f32[448,512]{1,0:T(8,128)S(1)} %get-tuple-element.29.bext_ref, bf16[448,128]{1,0:T(8,128)(2,1)S(1)} %get-tuple-element.30.a_ref, f32[8,512]{1,0:T(8,128)S(1)} %get-tuple-element.31.c_ref, bf16[32,144]{1,0:T(8,128)(2,1)S(1)} %pad_maximum_fusion.wfp_ref), custom_call_target="tpu_custom_call" | custom-call | flops 1577058304 | tf_op jit(solution)/shard_map/eps_part/pallas_call | solution.py:31
  230.7 12.2 %all_to_all.57.got_ref = bf16[32,16,128]{2,1,0:T(8,128)(2,1)S(1)} all-to-all(bf16[32,16,128]{2,1,0:T(8,128)(2,1)S(1)} %bitcast.27), channel_id=1, replica_groups=mesh['parts'=2,'zhi'=8,'zlo'=4,'frame'=4,'head'=2] {'frame','zlo','head'}, dimensions={0} | all-to-all | bytes 262144 | tf_op jit(solution)/shard_map/all_to_all | solution.py:570
  242.9 1.3 last.1
  244.1 12.2 %all_to_all.58.got_ref = f32[32,8,128]{2,1,0:T(8,128)S(1)} all-to-all(f32[32,8,128]{2,1,0:T(8,128)S(1)} %last.1), channel_id=1, replica_groups=mesh['parts'=2,'zhi'=8,'zlo'=4,'frame'=4,'head'=2] {'frame','zlo','head'}, dimensions={0} | all-to-all | bytes 262144 | tf_op jit(solution)/shard_map/all_to_all | solution.py:603
  256.3 1.4 end.1
  (8 shorter events, 0.1 us)
Async XLA Ops:
  18.9 4.7 %copy-start.9 = (bf16[127,128]{1,0:T(8,128)(2,1)S(1)}, bf16[127,128]{1,0:T(8,128)(2,1)}, u32[]{:S(2)}) copy-start(bf16[127,128]{1,0:T(8,128)(2,1)} %get-tuple-element.25) | copy-start | bytes 97540
  18.9 87.2 %all-to-all-start.1 = ((bf16[4,144,1152]{2,1,0:T(8,128)(2,1)}), bf16[4,144,1152]{2,1,0:T(8,128)(2,1)S(1)}, u32[]{:S(2)}, u32[]{:S(2)}) async-start(bf16[4,144,1152]{2,1,0:T(8,128)(2,1)} %get-tuple-element.27), calls=%async_computation.1 | async-start | bytes 2654208 | tf_op jit(solution)/shard_map/all_to_all | solution.py:524
  23.5 82.7 %copy-start = (bf16[128,1152]{1,0:T(8,128)(2,1)S(1)}, bf16[128,1152]{1,0:T(8,128)(2,1)}, u32[]{:S(2)}) copy-start(bf16[128,1152]{1,0:T(8,128)(2,1)} %position_ref.3) | copy-start | bytes 884740
  23.5 82.7 %copy-start.1 = (bf16[128,1152]{1,0:T(8,128)(2,1)S(1)}, bf16[128,1152]{1,0:T(8,128)(2,1)}, u32[]{:S(2)}) copy-start(bf16[128,1152]{1,0:T(8,128)(2,1)} %table_ref.1) | copy-start | bytes 884740
  23.5 82.7 %copy-start.2 = (bf16[16,1152]{1,0:T(8,128)(2,1)S(1)}, bf16[16,1152]{1,0:T(8,128)(2,1)}, u32[]{:S(2)}) copy-start(bf16[16,1152]{1,0:T(8,128)(2,1)} %final_ref.3) | copy-start | bytes 110596
  23.5 82.7 %copy-start.3 = (bf16[16,1152]{1,0:T(8,128)(2,1)S(1)}, bf16[16,1152]{1,0:T(8,128)(2,1)}, u32[]{:S(2)}) copy-start(bf16[16,1152]{1,0:T(8,128)(2,1)} %w_in_ref.1) | copy-start | bytes 110596
  23.5 82.7 %copy-start.4 = (f32[16,128]{1,0:T(8,128)S(1)}, f32[16,128]{1,0:T(8,128)}, u32[]{:S(2)}) copy-start(f32[16,128]{1,0:T(8,128)} %start_ref.3) | copy-start | bytes 24580
  23.5 82.7 %copy-start.5 = (s32[7]{0:T(128)S(1)}, s32[7]{0:T(128)}, u32[]{:S(2)}) copy-start(s32[7]{0:T(128)} %concatenate.7.where_ref) | copy-start | bytes 88
  23.5 82.7 %copy-start.6 = (f32[1152]{0:T(1024)S(1)}, f32[1152]{0:T(1024)}, u32[]{:S(2)}) copy-start(f32[1152]{0:T(1024)} %param.20) | copy-start | bytes 13828
  23.5 82.7 %copy-start.7 = (f32[128]{0:T(128)S(1)}, f32[128]{0:T(128)}, u32[]{:S(2)}) copy-start(f32[128]{0:T(128)} %param.17) | copy-start | bytes 1540
  23.6 82.7 %copy-start.8 = (f32[128]{0:T(128)S(1)}, f32[128]{0:T(128)}, u32[]{:S(2)}) copy-start(f32[128]{0:T(128)} %param.18) | copy-start | bytes 1540

commit v5 on v4

--- a/solution.py
+++ b/solution.py
@@ -191,14 +191,14 @@
                 send_ref[(frame * groups + group) * cores + core] = rounded
 
 
-def last_body(lat, frames, cores, where_ref, got_ref, x_ref, noise_ref, base_ref, fblk_ref,
+def last_body(lat, frames, cores, got_ref, x_ref, noise_ref, base_ref, fblk_ref,
               coef_ref, sq0_ref, sq1_ref, sq2_ref, send_ref):
     drifts, states, square = advance(
         lat, frames, cores, got_ref, x_ref, noise_ref, base_ref, fblk_ref, coef_ref
     )
     groups, rows, lanes = x_ref.shape
     half = rows // 2
-    zhi = where_ref[0]
+    zhi = lax.axis_index("zhi")
     width = groups * lat
     first = zhi * groups
     per_group = lanes // lat
@@ -221,10 +221,10 @@
                 send_ref[(frame * groups + group) * cores + core] = mixed
 
 
-def end_body(lat, frames, cores, cells, where_ref, got_ref, traj_ref, norm_ref):
+def end_body(lat, frames, cores, cells, got_ref, traj_ref, norm_ref):
     members, half, lanes = got_ref.shape
     groups = members // (frames * cores)
-    frame, zlo = where_ref[1], where_ref[2]
+    frame, zlo = lax.axis_index("frame"), lax.axis_index("zlo")
     width = groups * lat
     everyone = got_ref[0]
     for member in range(1, members):
@@ -243,20 +243,22 @@
     traj_ref[...] = jnp.concatenate(rows, axis=0).T[:lat, :]
 
 
-def smem_first(body, out_shape, where, *args, scratch=(), grant=GRANT, scalars=(), name=None):
+def smem_first(body, out_shape, *args, smem=0, scratch=(), grant=GRANT, scalars=(), flops=0, name=None):
     spec = pl.BlockSpec(memory_space=pltpu.VMEM)
+    held = pl.BlockSpec(memory_space=pltpu.SMEM)
     out_specs = jax.tree.map(lambda _: spec, out_shape)
     for at in scalars:
-        out_specs = (*out_specs[:at], pl.BlockSpec(memory_space=pltpu.SMEM), *out_specs[at + 1 :])
+        out_specs = (*out_specs[:at], held, *out_specs[at + 1 :])
     return pl.pallas_call(
         body,
         out_shape=out_shape,
-        in_specs=[pl.BlockSpec(memory_space=pltpu.SMEM)] + [spec] * len(args),
+        in_specs=[held] * smem + [spec] * (len(args) - smem),
         out_specs=out_specs,
         scratch_shapes=list(scratch),
+        cost_estimate=pl.CostEstimate(flops=flops, bytes_accessed=0, transcendentals=0),
         compiler_params=pltpu.CompilerParams(vmem_limit_bytes=grant),
         name=name,
-    )(where, *args)
+    )(*args)
 
 
 def split_two(a):
@@ -275,10 +277,10 @@
     return jnp.where(is_hi, hi, jnp.where(is_mid, mid, low)).astype(BF16)
 
 
-def prep_body(lat, cores, extra, where_ref, got_ref, all_ref, position_ref, start_ref, table_ref,
+def prep_body(lat, cores, extra, got_ref, all_ref, position_ref, start_ref, table_ref,
               gain_ref, keep_ref, rate_ref, w_in_ref, final_ref, bext_ref, a_ref, c_ref, base_ref, fblk_ref, coef_ref, noise_ref, state_ref, x_ref,
               temb_ref, turned_ref, w_ref, index_ref):
-    zlo, core = where_ref[2], where_ref[3]
+    zlo, core = lax.axis_index("zlo"), lax.axis_index("head")
     frames = all_ref.shape[0]
     rows, model = position_ref.shape
     groups, mine, lanes = base_ref.shape
@@ -407,20 +409,15 @@
     return jnp.dot(values, jnp.where(wanted, 1.0, 0.0).astype(BF16), preferred_element_type=F32)
 
 
-def pack_body(extra, where_ref, qkv_ref, proj_ref, final_ref, start_ref, position_ref,
-              mix_ref, frame_ref, main_ref, rows_ref, half_ref):
-    frame, step = where_ref[1], where_ref[4]
-    lat, rows = start_ref.shape
+def mix_body(proj_ref, final_ref, mix_ref):
+    frame = lax.axis_index("frame")
+    step = lax.axis_index("zhi") * lax.axis_size("zlo") + lax.axis_index("zlo")
+    lat, model = final_ref.shape
     rows_d, width = proj_ref.shape
-    frames, parts = frame_ref.shape[0], mix_ref.shape[0]
-    lanes = main_ref.shape[1]
-    cols = mix_ref.shape[2]
-    tall = rows_d // 2
-
+    parts, each, cols = mix_ref.shape
+    lanes = 128
     column = lax.broadcasted_iota(jnp.int32, (width, 2 * lanes), 0) - frame * cols
-    lane = lax.broadcasted_iota(jnp.int32, (width, 2 * lanes), 1)
-    both = column == lane
-    model = final_ref.shape[1]
+    both = column == lax.broadcasted_iota(jnp.int32, (width, 2 * lanes), 1)
     feature = lax.broadcasted_iota(jnp.int32, (model, lanes), 0) - step * rows_d
     final = exact_pick(final_ref[...], feature == lax.broadcasted_iota(jnp.int32, (model, lanes), 1))
     proj = exact_pick(proj_ref[...], both)
@@ -429,9 +426,23 @@
     feature_lane = lax.broadcasted_iota(jnp.int32, final.shape, 1)
     final = jnp.where(feature_lane < rows_d, final, 0.0).astype(BF16)
     mix = jnp.dot(final, proj, preferred_element_type=F32)
-    each = lat // parts
     for part in range(parts):
         mix_ref[part] = mix[part * each : (part + 1) * each, :cols]
+
+
+def pack_body(extra, cols, time_ref, plan_ref, qkv_ref, start_ref, position_ref,
+              frame_ref, main_ref, rows_ref, half_ref):
+    frame = lax.axis_index("frame")
+    lat, rows = start_ref.shape
+    rows_d, width = qkv_ref.shape[1:]
+    frames = frame_ref.shape[0]
+    lanes = main_ref.shape[1]
+    tall = rows_d // 2
+
+    column = lax.broadcasted_iota(jnp.int32, (width, 2 * lanes), 0) - frame * cols
+    lane = lax.broadcasted_iota(jnp.int32, (width, 2 * lanes), 1)
+    both = column == lane
+    model = position_ref.shape[1]
 
     noise = jnp.concatenate(
         [start_ref[...], jnp.zeros((lat, model - rows), F32)], axis=1
@@ -452,8 +463,8 @@
     half_ref[...] = side[:, lanes:]
     rows_ref[3 * rows_d : 3 * rows_d + tall, :] = side[:tall, :lanes] + half_ref[tall:, :]
     spot = lax.broadcasted_iota(jnp.int32, (1, lanes), 1)
-    times = where_ref[5].astype(F32)
-    plans = where_ref[6].astype(F32)
+    times = time_ref[0].astype(F32)
+    plans = plan_ref[0].astype(F32)
     rows_ref[3 * rows_d + tall : 3 * rows_d + tall + 1, :] = jnp.where(
         spot == 0, times, jnp.where(spot == 1, plans, 0.0)
     )
@@ -487,31 +498,34 @@
     members = frames * zlo_n * cores
     mine = tokens // members
     lanes = steps * lat
-    frame, zlo, zhi, core = (lax.axis_index(a) for a in ("frame", "zlo", "zhi", "head"))
-    step = zhi * zlo_n + zlo
-
-    where = jnp.concatenate(
-        [jnp.stack([zhi, frame, zlo, core, step]).astype(jnp.int32), time_index, sched_index]
-    )
+
     tall = rows_d // 2
     extra = cols - lanes
     pieces = cols // tall
     payload_rows = 3 * rows_d + tall + 1
-    mix, frame_load, payload = smem_first(
-        functools.partial(pack_body, extra),
+    mix = smem_first(
+        mix_body,
+        jax.ShapeDtypeStruct((zlo_n, lat // zlo_n, cols), F32),
+        w_proj,
+        w_final,
+        grant=None,
+        name="mix",
+    )
+    frame_load, payload = smem_first(
+        functools.partial(pack_body, extra, cols),
         (
-            jax.ShapeDtypeStruct((zlo_n, lat // zlo_n, cols), F32),
             jax.ShapeDtypeStruct((frames, row_count + lat, model), BF16),
             jax.ShapeDtypeStruct((payload_rows, lanes), BF16),
         ),
-        where,
+        time_index,
+        sched_index,
         w_qkv.transpose(1, 0, 2),
-        w_proj,
-        w_final,
         start_noise,
         position,
+        smem=2,
         scratch=(pltpu.VMEM((payload_rows + 1, lanes), F32), pltpu.VMEM((rows_d, lanes), F32)),
         grant=None,
+        flops=4_000_000_000,
         name="pack",
     )
 
@@ -544,7 +558,6 @@
             jax.ShapeDtypeStruct((zlo_n, mine, lanes), F32),
             jax.ShapeDtypeStruct((tokens, lanes), BF16),
         ),
-        where,
         gathered,
         frame_all,
         position,
@@ -590,8 +603,7 @@
             send = smem_first(
                 functools.partial(last_body, lat, frames, cores),
                 jax.ShapeDtypeStruct((members, mine // 2, lanes), F32),
-                where,
-                got,
+                        got,
                 states,
                 noise,
                 base,
@@ -607,7 +619,6 @@
             jax.ShapeDtypeStruct((lat, row_count), F32),
             jax.ShapeDtypeStruct((ITERS,), F32),
         ),
-        where,
         ended,
         scalars=(1,),
         name="end",

time: 258 us -> 255 us (0.988)
  blocking collectives: 209 us -> 196 us
  starting transfers between devices: 4.43 us -> 13.5 us
    all_to_all x1 -> x0, blocking collectives: 13.5 us -> none  [local(): mix = jnp.sum(lax.all_to_all(mix, 'zlo', 0, 0, tiled=True), axis=0)]
    all_to_all x0 -> x1, starting transfers between devices: none -> 9.02 us  [local(): mix = jnp.sum(lax.all_to_all(mix, 'zlo', 0, 0, tiled=True), axis=0)]
    pallas_call x4 -> x5, Pallas kernels: 8.91 us -> 8.72 us  [smem_first(): pl.pallas_call(body, out_shape=out_shape, in_specs=[held] * smem + [spec]...]
  transfers between devices with their start and end apart: 1 -> 2, of which waited for: 0 -> 1; matrix products, arithmetic and copies ran while one was open for 0% -> 0% of each run, Pallas kernels for 0% -> 1%
where the time goes in v5:
time: 255 us; the launch traced here: 254 us
  blocking collectives  196 us (77%)
  Pallas kernels  40.4 us (16%)
  starting transfers between devices  13.5 us (5%)
    all_gather x1, blocking collectives, local(): gathered = lax.all_gather(payload, STEP, axis=0)  83.5 us
    all_to_all x4, blocking collectives, local(): lax.all_to_all(part_eps.reshape(members, mine, lanes), HOOD, 0, 0, tiled=...  64.1 us
    all_to_all x3, blocking collectives, local(): x = lax.all_to_all(send, HOOD, 0, 0, tiled=True).reshape(tokens, lanes)  36.5 us
    pallas_call x7, Pallas kernels, vmem_call(): pl.pallas_call(body, out_shape=out_shape, in_specs=[spec] * len(args), ou...  31.7 us
    all_to_all x1, blocking collectives, local(): ended = lax.all_to_all(send, HOOD, 0, 0, tiled=True)  12.2 us
    all_to_all x1, starting transfers between devices, local(): mix = jnp.sum(lax.all_to_all(mix, 'zlo', 0, 0, tiled=True), axis=0)  9.02 us
    pallas_call x5, Pallas kernels, smem_first(): pl.pallas_call(body, out_shape=out_shape, in_specs=[held] * smem + [spec]...  8.72 us
  transfers between devices with their start and end apart: 2, of which 1 were waited for; matrix products, arithmetic and copies ran while one was open for 0% of the time, Pallas kernels for 1%

profile of v5, /device:TPU:33, one launch (start us, length us, event | category | flops | bytes accessed | tf_op | source)
XLA Modules:
  0.0 254.0 jit_solution(6089660476434024112)
XLA Ops:
  0.6 1.8 mix.1
  2.4 9.0 %all-to-all-start = ((f32[4,4,144]{2,1,0:T(4,128)}), f32[4,4,144]{2,1,0:T(4,128)S(1)}, u32[]{:S(2)}, u32[]{:S(2)}) async-start(f32[4,4,144]{2,1,0:T(4,128)} %mix.1), calls=%async_computation | async-start | bytes 32768 | tf_op jit(solution)/shard_map/all_to_all | solution.py:532
  12.7 2.6 %pack.1 = (bf16[4,144,1152]{2,1,0:T(8,128)(2,1)}, bf16[127,128]{1,0:T(8,128)(2,1)}) custom-call(s32[1]{0:T(128)S(6)} %copy.22.time_ref, s32[1]{0:T(128)S(6)} %copy.23.plan_ref, bf16[3,36,576]{2,1,0:T(8,128)(2,1)} %bitcast.35, f32[16,128]{1,0:T(8,128)} %start_ref.3, bf16[128,1152]{1,0:T(8,128)(2,1)} %position_ref.3), custom_call_target="tpu_custom_call" | custom-call | flops 4000000000 | tf_op jit(solution)/shard_map/pack/pallas_call | solution.py:252
  15.3 0.5 all-to-all-done
  15.9 4.4 %all-to-all-start.1 = ((bf16[4,144,1152]{2,1,0:T(8,128)(2,1)}), bf16[4,144,1152]{2,1,0:T(8,128)(2,1)S(1)}, u32[]{:S(2)}, u32[]{:S(2)}) async-start(bf16[4,144,1152]{2,1,0:T(8,128)(2,1)} %get-tuple-element.25), calls=%async_computation.1 | async-start | bytes 2654208 | tf_op jit(solution)/shard_map/all_to_all | solution.py:538
  20.3 0.1 convert_element_type.17
  20.4 0.0 copy-start.1
  20.4 0.0 copy-start.2
  20.4 0.0 copy-start.3
  20.5 0.0 copy-start.4
  20.5 0.0 copy-start.5
  20.5 0.0 copy-start.6
  20.5 0.0 copy-start.7
  20.5 0.1 copy.18
  20.6 0.0 copy-done.8
  20.6 0.1 add_bitcast_fusion
  20.7 83.5 %all-gather.1.got_ref = bf16[32,127,128]{2,1,0:T(8,128)(2,1)S(1)} all-gather(bf16[1,127,128]{2,1,0:T(8,128)(2,1)S(1)} %add_bitcast_fusion), channel_id=2, replica_groups=mesh['parts'=2,'zhi'=8,'zlo'=4,'frame'=4,'head'=2] {'zhi','zlo'}, dimensions={0}, use_global_device_ids=true | all-gather | bytes 1072896 | tf_op jit(solution)/shard_map/all_gather | solution.py:540
  104.2 0.1 slice.6
  104.3 0.3 copy.21
  104.6 0.2 convert_reduce_fusion
  104.8 0.1 reshape.44
  104.9 0.0 all-to-all-done.1.all_ref
  104.9 0.0 copy-done
  104.9 0.0 copy-done.1
  104.9 0.0 copy-done.2
  104.9 0.0 copy-done.3
  105.0 0.0 copy-done.4
  105.0 0.0 copy-done.5
  105.0 0.0 copy-done.6
  105.0 0.0 copy-done.7
  105.0 2.8 %prep.1 = (f32[448,512]{1,0:T(8,128)S(1)}, bf16[448,128]{1,0:T(8,128)(2,1)S(1)}, f32[8,512]{1,0:T(8,128)S(1)}, f32[4,16,128]{2,1,0:T(8,128)S(1)}, bf16[384,128]{...) custom-call(bf16[32,127,128]{2,1,0:T(8,128)(2,1)S(1)} %all-gather.1., ...), custom_call_target="tpu_custom_call" | custom-call | tf_op jit(solution)/shard_map/prep/pallas_call | solution.py:252
  107.8 7.5 %eps_part.4 = bf16[512,128]{1,0:T(8,128)(2,1)S(1)} custom-call(bf16[512,128]{1,0:T(8,128)(2,1)S(1)} %get-tuple-element.26.x_ref, f32[448,512]{1,0:T(8,128)S(1)} %get-tuple-element.27.bext_ref, bf16[448,128]{1,0:T(8,128)(2,1)S(1)} %get-tuple-element.28.a_ref, f32[8,512]{1,0:T(8,128)S(1)} %get-tuple-element.29.c_ref, bf16[32,144]{1,0:T(8,128)(2,1)S(1)} %pad_maximum_fusion.wfp_ref), custom_call_target="tpu_custom_call" | custom-call | flops 1577058304 | tf_op jit(solution)/shard_map/eps_part/pallas_call | solution.py:31
  115.3 27.5 %all_to_all.50.got_ref = bf16[32,16,128]{2,1,0:T(8,128)(2,1)S(1)} all-to-all(bf16[32,16,128]{2,1,0:T(8,128)(2,1)S(1)} %bitcast.23), channel_id=1, replica_groups=mesh['parts'=2,'zhi'=8,'zlo'=4,'frame'=4,'head'=2] {'frame','zlo','head'}, dimensions={0} | all-to-all | bytes 262144 | tf_op jit(solution)/shard_map/all_to_all | solution.py:583
  142.8 0.6 advance.3
  143.4 12.2 %all_to_all.51 = bf16[32,16,128]{2,1,0:T(8,128)(2,1)S(1)} all-to-all(bf16[32,16,128]{2,1,0:T(8,128)(2,1)S(1)} %get-tuple-element.35), channel_id=1, replica_groups=mesh['parts'=2,'zhi'=8,'zlo'=4,'frame'=4,'head'=2] {'frame','zlo','head'}, dimensions={0} | all-to-all | bytes 262144 | tf_op jit(solution)/shard_map/all_to_all | solution.py:601
  155.6 7.5 %eps_part.5 = bf16[512,128]{1,0:T(8,128)(2,1)S(1)} custom-call(bf16[512,128]{1,0:T(8,128)(2,1)S(1)} %bitcast.24, f32[448,512]{1,0:T(8,128)S(1)} %get-tuple-element.27.bext_ref, bf16[448,128]{1,0:T(8,128)(2,1)S(1)} %get-tuple-element.28.a_ref, f32[8,512]{1,0:T(8,128)S(1)} %get-tuple-element.29.c_ref, bf16[32,144]{1,0:T(8,128)(2,1)S(1)} %pad_maximum_fusion.wfp_ref), custom_call_target="tpu_custom_call" | custom-call | flops 1577058304 | tf_op jit(solution)/shard_map/eps_part/pallas_call | solution.py:31
  163.1 12.2 %all_to_all.52.got_ref = bf16[32,16,128]{2,1,0:T(8,128)(2,1)S(1)} all-to-all(bf16[32,16,128]{2,1,0:T(8,128)(2,1)S(1)} %bitcast.25), channel_id=1, replica_groups=mesh['parts'=2,'zhi'=8,'zlo'=4,'frame'=4,'head'=2] {'frame','zlo','head'}, dimensions={0} | all-to-all | bytes 262144 | tf_op jit(solution)/shard_map/all_to_all | solution.py:583
  175.2 0.6 advance.4
  175.8 12.2 %all_to_all.53 = bf16[32,16,128]{2,1,0:T(8,128)(2,1)S(1)} all-to-all(bf16[32,16,128]{2,1,0:T(8,128)(2,1)S(1)} %get-tuple-element.37), channel_id=1, replica_groups=mesh['parts'=2,'zhi'=8,'zlo'=4,'frame'=4,'head'=2] {'frame','zlo','head'}, dimensions={0} | all-to-all | bytes 262144 | tf_op jit(solution)/shard_map/all_to_all | solution.py:601
  188.0 7.5 %eps_part.6 = bf16[512,128]{1,0:T(8,128)(2,1)S(1)} custom-call(bf16[512,128]{1,0:T(8,128)(2,1)S(1)} %bitcast.26, f32[448,512]{1,0:T(8,128)S(1)} %get-tuple-element.27.bext_ref, bf16[448,128]{1,0:T(8,128)(2,1)S(1)} %get-tuple-element.28.a_ref, f32[8,512]{1,0:T(8,128)S(1)} %get-tuple-element.29.c_ref, bf16[32,144]{1,0:T(8,128)(2,1)S(1)} %pad_maximum_fusion.wfp_ref), custom_call_target="tpu_custom_call" | custom-call | flops 1577058304 | tf_op jit(solution)/shard_map/eps_part/pallas_call | solution.py:31
  195.5 12.2 %all_to_all.54.got_ref = bf16[32,16,128]{2,1,0:T(8,128)(2,1)S(1)} all-to-all(bf16[32,16,128]{2,1,0:T(8,128)(2,1)S(1)} %bitcast.27), channel_id=1, replica_groups=mesh['parts'=2,'zhi'=8,'zlo'=4,'frame'=4,'head'=2] {'frame','zlo','head'}, dimensions={0} | all-to-all | bytes 262144 | tf_op jit(solution)/shard_map/all_to_all | solution.py:583
  207.6 0.6 advance.5
  208.2 12.2 %all_to_all.55 = bf16[32,16,128]{2,1,0:T(8,128)(2,1)S(1)} all-to-all(bf16[32,16,128]{2,1,0:T(8,128)(2,1)S(1)} %get-tuple-element.39), channel_id=1, replica_groups=mesh['parts'=2,'zhi'=8,'zlo'=4,'frame'=4,'head'=2] {'frame','zlo','head'}, dimensions={0} | all-to-all | bytes 262144 | tf_op jit(solution)/shard_map/all_to_all | solution.py:601
  220.4 7.5 %eps_part.7 = bf16[512,128]{1,0:T(8,128)(2,1)S(1)} custom-call(bf16[512,128]{1,0:T(8,128)(2,1)S(1)} %bitcast.21, f32[448,512]{1,0:T(8,128)S(1)} %get-tuple-element.27.bext_ref, bf16[448,128]{1,0:T(8,128)(2,1)S(1)} %get-tuple-element.28.a_ref, f32[8,512]{1,0:T(8,128)S(1)} %get-tuple-element.29.c_ref, bf16[32,144]{1,0:T(8,128)(2,1)S(1)} %pad_maximum_fusion.wfp_ref), custom_call_target="tpu_custom_call" | custom-call | flops 1577058304 | tf_op jit(solution)/shard_map/eps_part/pallas_call | solution.py:31
  227.9 12.2 %all_to_all.56.got_ref = bf16[32,16,128]{2,1,0:T(8,128)(2,1)S(1)} all-to-all(bf16[32,16,128]{2,1,0:T(8,128)(2,1)S(1)} %bitcast.22), channel_id=1, replica_groups=mesh['parts'=2,'zhi'=8,'zlo'=4,'frame'=4,'head'=2] {'frame','zlo','head'}, dimensions={0} | all-to-all | bytes 262144 | tf_op jit(solution)/shard_map/all_to_all | solution.py:583
  240.1 0.7 last.1
  240.8 12.2 %all_to_all.57.got_ref = f32[32,8,128]{2,1,0:T(8,128)S(1)} all-to-all(f32[32,8,128]{2,1,0:T(8,128)S(1)} %last.1), channel_id=1, replica_groups=mesh['parts'=2,'zhi'=8,'zlo'=4,'frame'=4,'head'=2] {'frame','zlo','head'}, dimensions={0} | all-to-all | bytes 262144 | tf_op jit(solution)/shard_map/all_to_all | solution.py:615
  253.0 0.8 end.1
  (7 shorter events, 0.0 us)
Async XLA Ops:
  2.4 13.5 %all-to-all-start = ((f32[4,4,144]{2,1,0:T(4,128)}), f32[4,4,144]{2,1,0:T(4,128)S(1)}, u32[]{:S(2)}, u32[]{:S(2)}) async-start(f32[4,4,144]{2,1,0:T(4,128)} %mix.1), calls=%async_computation | async-start | bytes 32768 | tf_op jit(solution)/shard_map/all_to_all | solution.py:532
  15.9 4.7 %copy-start.8 = (bf16[127,128]{1,0:T(8,128)(2,1)S(1)}, bf16[127,128]{1,0:T(8,128)(2,1)}, u32[]{:S(2)}) copy-start(bf16[127,128]{1,0:T(8,128)(2,1)} %get-tuple-element.24) | copy-start | bytes 97540
  15.9 89.0 %all-to-all-start.1 = ((bf16[4,144,1152]{2,1,0:T(8,128)(2,1)}), bf16[4,144,1152]{2,1,0:T(8,128)(2,1)S(1)}, u32[]{:S(2)}, u32[]{:S(2)}) async-start(bf16[4,144,1152]{2,1,0:T(8,128)(2,1)} %get-tuple-element.25), calls=%async_computation.1 | async-start | bytes 2654208 | tf_op jit(solution)/shard_map/all_to_all | solution.py:538
  20.4 84.5 %copy-start = (bf16[128,1152]{1,0:T(8,128)(2,1)S(1)}, bf16[128,1152]{1,0:T(8,128)(2,1)}, u32[]{:S(2)}) copy-start(bf16[128,1152]{1,0:T(8,128)(2,1)} %position_ref.3) | copy-start | bytes 884740
  20.4 84.5 %copy-start.1 = (bf16[128,1152]{1,0:T(8,128)(2,1)S(1)}, bf16[128,1152]{1,0:T(8,128)(2,1)}, u32[]{:S(2)}) copy-start(bf16[128,1152]{1,0:T(8,128)(2,1)} %table_ref.1) | copy-start | bytes 884740
  20.4 84.5 %copy-start.2 = (bf16[16,1152]{1,0:T(8,128)(2,1)S(1)}, bf16[16,1152]{1,0:T(8,128)(2,1)}, u32[]{:S(2)}) copy-start(bf16[16,1152]{1,0:T(8,128)(2,1)} %final_ref.3) | copy-start | bytes 110596
  20.4 84.5 %copy-start.3 = (bf16[16,1152]{1,0:T(8,128)(2,1)S(1)}, bf16[16,1152]{1,0:T(8,128)(2,1)}, u32[]{:S(2)}) copy-start(bf16[16,1152]{1,0:T(8,128)(2,1)} %w_in_ref.1) | copy-start | bytes 110596
  20.5 84.5 %copy-start.4 = (f32[16,128]{1,0:T(8,128)S(1)}, f32[16,128]{1,0:T(8,128)}, u32[]{:S(2)}) copy-start(f32[16,128]{1,0:T(8,128)} %start_ref.3) | copy-start | bytes 24580
  20.5 84.5 %copy-start.5 = (f32[1152]{0:T(1024)S(1)}, f32[1152]{0:T(1024)}, u32[]{:S(2)}) copy-start(f32[1152]{0:T(1024)} %param.20) | copy-start | bytes 13828
  20.5 84.5 %copy-start.6 = (f32[128]{0:T(128)S(1)}, f32[128]{0:T(128)}, u32[]{:S(2)}) copy-start(f32[128]{0:T(128)} %param.17) | copy-start | bytes 1540
  20.5 84.5 %copy-start.7 = (f32[128]{0:T(128)S(1)}, f32[128]{0:T(128)}, u32[]{:S(2)}) copy-start(f32[128]{0:T(128)} %param.18) | copy-start | bytes 1540

commit v6 on v5

--- a/solution.py
+++ b/solution.py
@@ -451,17 +451,16 @@
         frame_ref[at, :rows] = position_ref[...]
         frame_ref[at, rows:] = noise
 
-    side = jnp.zeros((rows_d, 2 * lanes), F32)
+    side = jnp.zeros(half_ref.shape, F32)
+    place = lax.broadcasted_iota(jnp.int32, half_ref.shape, 1)
     for part in range(3):
-        weights = qkv_ref[part]
-        rows_ref[part * rows_d : (part + 1) * rows_d, :] = exact_pick(weights, both)[:, :lanes]
-        shifted = lane - part * extra
-        first = (column - lanes == shifted) & (shifted >= 0) & (shifted < extra)
-        shifted = lane - lanes - (3 + part) * extra
-        second = (column - lanes == shifted) & (shifted >= 0) & (shifted < extra)
-        side = side + exact_pick(weights, first | second)
-    half_ref[...] = side[:, lanes:]
-    rows_ref[3 * rows_d : 3 * rows_d + tall, :] = side[:tall, :lanes] + half_ref[tall:, :]
+        picked = exact_pick(qkv_ref[part], both)
+        rows_ref[part * rows_d : (part + 1) * rows_d, :] = picked[:, :lanes]
+        half_ref[:rows_d, :] = picked[:, lanes:]
+        rest = jnp.where(place < extra, half_ref[...], 0.0)
+        side = side + (pltpu.roll(rest, part * extra, 1) if part else rest)
+    half_ref[...] = pltpu.roll(side, 3 * extra, 1)
+    rows_ref[3 * rows_d : 3 * rows_d + tall, :] = side[:tall] + half_ref[tall:rows_d, :]
     spot = lax.broadcasted_iota(jnp.int32, (1, lanes), 1)
     times = time_ref[0].astype(F32)
     plans = plan_ref[0].astype(F32)
@@ -523,7 +522,7 @@
         start_noise,
         position,
         smem=2,
-        scratch=(pltpu.VMEM((payload_rows + 1, lanes), F32), pltpu.VMEM((rows_d, lanes), F32)),
+        scratch=(pltpu.VMEM((payload_rows + 1, lanes), F32), pltpu.VMEM((rows_d + 4, lanes), F32)),
         grant=None,
         flops=4_000_000_000,
         name="pack",

time: 255 us -> 255 us (level)
  no operation moved by 1% of the time
where the time goes in v6:
time: 255 us; the launch traced here: 254 us
  blocking collectives  196 us (77%)
  Pallas kernels  40.3 us (16%)
  starting transfers between devices  13.5 us (5%)
    all_gather x1, blocking collectives, local(): gathered = lax.all_gather(payload, STEP, axis=0)  83.4 us
    all_to_all x4, blocking collectives, local(): lax.all_to_all(part_eps.reshape(members, mine, lanes), HOOD, 0, 0, tiled=...  64 us
    all_to_all x3, blocking collectives, local(): x = lax.all_to_all(send, HOOD, 0, 0, tiled=True).reshape(tokens, lanes)  36.5 us
    pallas_call x7, Pallas kernels, vmem_call(): pl.pallas_call(body, out_shape=out_shape, in_specs=[spec] * len(args), ou...  31.7 us
    all_to_all x1, blocking collectives, local(): ended = lax.all_to_all(send, HOOD, 0, 0, tiled=True)  12.2 us
    all_to_all x1, starting transfers between devices, local(): mix = jnp.sum(lax.all_to_all(mix, 'zlo', 0, 0, tiled=True), axis=0)  9.02 us
    pallas_call x5, Pallas kernels, smem_first(): pl.pallas_call(body, out_shape=out_shape, in_specs=[held] * smem + [spec]...  8.61 us
  transfers between devices with their start and end apart: 2, of which 1 were waited for; matrix products, arithmetic and copies ran while one was open for 0% of the time, Pallas kernels for 1%

profile of v6, /device:TPU:33, one launch (start us, length us, event | category | flops | bytes accessed | tf_op | source)
XLA Modules:
  0.0 253.9 jit_solution(3032796336098688953)
XLA Ops:
  0.6 1.8 mix.1
  2.4 9.0 %all-to-all-start = ((f32[4,4,144]{2,1,0:T(4,128)}), f32[4,4,144]{2,1,0:T(4,128)S(1)}, u32[]{:S(2)}, u32[]{:S(2)}) async-start(f32[4,4,144]{2,1,0:T(4,128)} %mix.1), calls=%async_computation | async-start | bytes 32768 | tf_op jit(solution)/shard_map/all_to_all | solution.py:531
  12.7 2.5 pack.1
  15.2 0.6 all-to-all-done
  15.9 4.4 %all-to-all-start.1 = ((bf16[4,144,1152]{2,1,0:T(8,128)(2,1)}), bf16[4,144,1152]{2,1,0:T(8,128)(2,1)S(1)}, u32[]{:S(2)}, u32[]{:S(2)}) async-start(bf16[4,144,1152]{2,1,0:T(8,128)(2,1)} %get-tuple-element.25), calls=%async_computation.1 | async-start | bytes 2654208 | tf_op jit(solution)/shard_map/all_to_all | solution.py:537
  20.3 0.1 convert_element_type.17
  20.4 0.0 copy-start.1
  20.4 0.0 copy-start.2
  20.4 0.0 copy-start.3
  20.5 0.0 copy-start.4
  20.5 0.0 copy-start.5
  20.5 0.0 copy-start.6
  20.5 0.0 copy-start.7
  20.5 0.1 copy.18
  20.6 0.0 copy-done.8
  20.6 0.1 add_bitcast_fusion
  20.7 83.4 %all-gather.1.got_ref = bf16[32,127,128]{2,1,0:T(8,128)(2,1)S(1)} all-gather(bf16[1,127,128]{2,1,0:T(8,128)(2,1)S(1)} %add_bitcast_fusion), channel_id=2, replica_groups=mesh['parts'=2,'zhi'=8,'zlo'=4,'frame'=4,'head'=2] {'zhi','zlo'}, dimensions={0}, use_global_device_ids=true | all-gather | bytes 1072896 | tf_op jit(solution)/shard_map/all_gather | solution.py:539
  104.1 0.1 slice.6
  104.2 0.3 copy.21
  104.5 0.2 convert_reduce_fusion
  104.7 0.1 reshape.44
  104.8 0.0 all-to-all-done.1.all_ref
  104.8 0.0 copy-done
  104.8 0.0 copy-done.1
  104.8 0.0 copy-done.2
  104.8 0.0 copy-done.3
  104.8 0.0 copy-done.4
  104.9 0.0 copy-done.5
  104.9 0.0 copy-done.6
  104.9 0.0 copy-done.7
  104.9 2.8 %prep.1 = (f32[448,512]{1,0:T(8,128)S(1)}, bf16[448,128]{1,0:T(8,128)(2,1)S(1)}, f32[8,512]{1,0:T(8,128)S(1)}, f32[4,16,128]{2,1,0:T(8,128)S(1)}, bf16[384,128]{...) custom-call(bf16[32,127,128]{2,1,0:T(8,128)(2,1)S(1)} %all-gather.1., ...), custom_call_target="tpu_custom_call" | custom-call | tf_op jit(solution)/shard_map/prep/pallas_call | solution.py:252
  107.7 7.5 %eps_part.4 = bf16[512,128]{1,0:T(8,128)(2,1)S(1)} custom-call(bf16[512,128]{1,0:T(8,128)(2,1)S(1)} %get-tuple-element.26.x_ref, f32[448,512]{1,0:T(8,128)S(1)} %get-tuple-element.27.bext_ref, bf16[448,128]{1,0:T(8,128)(2,1)S(1)} %get-tuple-element.28.a_ref, f32[8,512]{1,0:T(8,128)S(1)} %get-tuple-element.29.c_ref, bf16[32,144]{1,0:T(8,128)(2,1)S(1)} %pad_maximum_fusion.wfp_ref), custom_call_target="tpu_custom_call" | custom-call | flops 1577058304 | tf_op jit(solution)/shard_map/eps_part/pallas_call | solution.py:31
  115.2 27.5 %all_to_all.50.got_ref = bf16[32,16,128]{2,1,0:T(8,128)(2,1)S(1)} all-to-all(bf16[32,16,128]{2,1,0:T(8,128)(2,1)S(1)} %bitcast.23), channel_id=1, replica_groups=mesh['parts'=2,'zhi'=8,'zlo'=4,'frame'=4,'head'=2] {'frame','zlo','head'}, dimensions={0} | all-to-all | bytes 262144 | tf_op jit(solution)/shard_map/all_to_all | solution.py:582
  142.7 0.6 advance.3
  143.3 12.2 %all_to_all.51 = bf16[32,16,128]{2,1,0:T(8,128)(2,1)S(1)} all-to-all(bf16[32,16,128]{2,1,0:T(8,128)(2,1)S(1)} %get-tuple-element.35), channel_id=1, replica_groups=mesh['parts'=2,'zhi'=8,'zlo'=4,'frame'=4,'head'=2] {'frame','zlo','head'}, dimensions={0} | all-to-all | bytes 262144 | tf_op jit(solution)/shard_map/all_to_all | solution.py:600
  155.5 7.5 %eps_part.5 = bf16[512,128]{1,0:T(8,128)(2,1)S(1)} custom-call(bf16[512,128]{1,0:T(8,128)(2,1)S(1)} %bitcast.24, f32[448,512]{1,0:T(8,128)S(1)} %get-tuple-element.27.bext_ref, bf16[448,128]{1,0:T(8,128)(2,1)S(1)} %get-tuple-element.28.a_ref, f32[8,512]{1,0:T(8,128)S(1)} %get-tuple-element.29.c_ref, bf16[32,144]{1,0:T(8,128)(2,1)S(1)} %pad_maximum_fusion.wfp_ref), custom_call_target="tpu_custom_call" | custom-call | flops 1577058304 | tf_op jit(solution)/shard_map/eps_part/pallas_call | solution.py:31
  162.9 12.2 %all_to_all.52.got_ref = bf16[32,16,128]{2,1,0:T(8,128)(2,1)S(1)} all-to-all(bf16[32,16,128]{2,1,0:T(8,128)(2,1)S(1)} %bitcast.25), channel_id=1, replica_groups=mesh['parts'=2,'zhi'=8,'zlo'=4,'frame'=4,'head'=2] {'frame','zlo','head'}, dimensions={0} | all-to-all | bytes 262144 | tf_op jit(solution)/shard_map/all_to_all | solution.py:582
  175.1 0.6 advance.4
  175.7 12.2 %all_to_all.53 = bf16[32,16,128]{2,1,0:T(8,128)(2,1)S(1)} all-to-all(bf16[32,16,128]{2,1,0:T(8,128)(2,1)S(1)} %get-tuple-element.37), channel_id=1, replica_groups=mesh['parts'=2,'zhi'=8,'zlo'=4,'frame'=4,'head'=2] {'frame','zlo','head'}, dimensions={0} | all-to-all | bytes 262144 | tf_op jit(solution)/shard_map/all_to_all | solution.py:600
  187.9 7.5 %eps_part.6 = bf16[512,128]{1,0:T(8,128)(2,1)S(1)} custom-call(bf16[512,128]{1,0:T(8,128)(2,1)S(1)} %bitcast.26, f32[448,512]{1,0:T(8,128)S(1)} %get-tuple-element.27.bext_ref, bf16[448,128]{1,0:T(8,128)(2,1)S(1)} %get-tuple-element.28.a_ref, f32[8,512]{1,0:T(8,128)S(1)} %get-tuple-element.29.c_ref, bf16[32,144]{1,0:T(8,128)(2,1)S(1)} %pad_maximum_fusion.wfp_ref), custom_call_target="tpu_custom_call" | custom-call | flops 1577058304 | tf_op jit(solution)/shard_map/eps_part/pallas_call | solution.py:31
  195.4 12.2 %all_to_all.54.got_ref = bf16[32,16,128]{2,1,0:T(8,128)(2,1)S(1)} all-to-all(bf16[32,16,128]{2,1,0:T(8,128)(2,1)S(1)} %bitcast.27), channel_id=1, replica_groups=mesh['parts'=2,'zhi'=8,'zlo'=4,'frame'=4,'head'=2] {'frame','zlo','head'}, dimensions={0} | all-to-all | bytes 262144 | tf_op jit(solution)/shard_map/all_to_all | solution.py:582
  207.5 0.6 advance.5
  208.1 12.2 %all_to_all.55 = bf16[32,16,128]{2,1,0:T(8,128)(2,1)S(1)} all-to-all(bf16[32,16,128]{2,1,0:T(8,128)(2,1)S(1)} %get-tuple-element.39), channel_id=1, replica_groups=mesh['parts'=2,'zhi'=8,'zlo'=4,'frame'=4,'head'=2] {'frame','zlo','head'}, dimensions={0} | all-to-all | bytes 262144 | tf_op jit(solution)/shard_map/all_to_all | solution.py:600
  220.3 7.5 %eps_part.7 = bf16[512,128]{1,0:T(8,128)(2,1)S(1)} custom-call(bf16[512,128]{1,0:T(8,128)(2,1)S(1)} %bitcast.21, f32[448,512]{1,0:T(8,128)S(1)} %get-tuple-element.27.bext_ref, bf16[448,128]{1,0:T(8,128)(2,1)S(1)} %get-tuple-element.28.a_ref, f32[8,512]{1,0:T(8,128)S(1)} %get-tuple-element.29.c_ref, bf16[32,144]{1,0:T(8,128)(2,1)S(1)} %pad_maximum_fusion.wfp_ref), custom_call_target="tpu_custom_call" | custom-call | flops 1577058304 | tf_op jit(solution)/shard_map/eps_part/pallas_call | solution.py:31
  227.8 12.2 %all_to_all.56.got_ref = bf16[32,16,128]{2,1,0:T(8,128)(2,1)S(1)} all-to-all(bf16[32,16,128]{2,1,0:T(8,128)(2,1)S(1)} %bitcast.22), channel_id=1, replica_groups=mesh['parts'=2,'zhi'=8,'zlo'=4,'frame'=4,'head'=2] {'frame','zlo','head'}, dimensions={0} | all-to-all | bytes 262144 | tf_op jit(solution)/shard_map/all_to_all | solution.py:582
  240.0 0.7 last.1
  240.7 12.2 %all_to_all.57.got_ref = f32[32,8,128]{2,1,0:T(8,128)S(1)} all-to-all(f32[32,8,128]{2,1,0:T(8,128)S(1)} %last.1), channel_id=1, replica_groups=mesh['parts'=2,'zhi'=8,'zlo'=4,'frame'=4,'head'=2] {'frame','zlo','head'}, dimensions={0} | all-to-all | bytes 262144 | tf_op jit(solution)/shard_map/all_to_all | solution.py:614
  252.9 0.8 end.1
  (7 shorter events, 0.0 us)
Async XLA Ops:
  2.4 13.5 %all-to-all-start = ((f32[4,4,144]{2,1,0:T(4,128)}), f32[4,4,144]{2,1,0:T(4,128)S(1)}, u32[]{:S(2)}, u32[]{:S(2)}) async-start(f32[4,4,144]{2,1,0:T(4,128)} %mix.1), calls=%async_computation | async-start | bytes 32768 | tf_op jit(solution)/shard_map/all_to_all | solution.py:531
  15.9 4.7 %copy-start.8 = (bf16[127,128]{1,0:T(8,128)(2,1)S(1)}, bf16[127,128]{1,0:T(8,128)(2,1)}, u32[]{:S(2)}) copy-start(bf16[127,128]{1,0:T(8,128)(2,1)} %get-tuple-element.24) | copy-start | bytes 97540
  15.9 88.9 %all-to-all-start.1 = ((bf16[4,144,1152]{2,1,0:T(8,128)(2,1)}), bf16[4,144,1152]{2,1,0:T(8,128)(2,1)S(1)}, u32[]{:S(2)}, u32[]{:S(2)}) async-start(bf16[4,144,1152]{2,1,0:T(8,128)(2,1)} %get-tuple-element.25), calls=%async_computation.1 | async-start | bytes 2654208 | tf_op jit(solution)/shard_map/all_to_all | solution.py:537
  20.4 84.4 %copy-start = (bf16[128,1152]{1,0:T(8,128)(2,1)S(1)}, bf16[128,1152]{1,0:T(8,128)(2,1)}, u32[]{:S(2)}) copy-start(bf16[128,1152]{1,0:T(8,128)(2,1)} %position_ref.3) | copy-start | bytes 884740
  20.4 84.4 %copy-start.1 = (bf16[128,1152]{1,0:T(8,128)(2,1)S(1)}, bf16[128,1152]{1,0:T(8,128)(2,1)}, u32[]{:S(2)}) copy-start(bf16[128,1152]{1,0:T(8,128)(2,1)} %table_ref.1) | copy-start | bytes 884740
  20.4 84.4 %copy-start.2 = (bf16[16,1152]{1,0:T(8,128)(2,1)S(1)}, bf16[16,1152]{1,0:T(8,128)(2,1)}, u32[]{:S(2)}) copy-start(bf16[16,1152]{1,0:T(8,128)(2,1)} %final_ref.3) | copy-start | bytes 110596
  20.4 84.4 %copy-start.3 = (bf16[16,1152]{1,0:T(8,128)(2,1)S(1)}, bf16[16,1152]{1,0:T(8,128)(2,1)}, u32[]{:S(2)}) copy-start(bf16[16,1152]{1,0:T(8,128)(2,1)} %w_in_ref.1) | copy-start | bytes 110596
  20.5 84.4 %copy-start.4 = (f32[16,128]{1,0:T(8,128)S(1)}, f32[16,128]{1,0:T(8,128)}, u32[]{:S(2)}) copy-start(f32[16,128]{1,0:T(8,128)} %start_ref.3) | copy-start | bytes 24580
  20.5 84.4 %copy-start.5 = (f32[1152]{0:T(1024)S(1)}, f32[1152]{0:T(1024)}, u32[]{:S(2)}) copy-start(f32[1152]{0:T(1024)} %param.20) | copy-start | bytes 13828
  20.5 84.4 %copy-start.6 = (f32[128]{0:T(128)S(1)}, f32[128]{0:T(128)}, u32[]{:S(2)}) copy-start(f32[128]{0:T(128)} %param.17) | copy-start | bytes 1540
  20.5 84.4 %copy-start.7 = (f32[128]{0:T(128)S(1)}, f32[128]{0:T(128)}, u32[]{:S(2)}) copy-start(f32[128]{0:T(128)} %param.18) | copy-start | bytes 1540
